TPU v7x, 32 devices: a whole 2x2x4 slice. The times are simulated.
32 devices in a mesh: section: 8 (over z, y), dp: 2 (over x), spatial: 2 (over core).
Axes of the slice: x: 2, y: 2, z: 4, core: 2. Of those that a mesh axis runs over, the one named last changes fastest.
Arguments:
- inbox: bfloat16 [8, 4, 2, 256, 4, 128], P('section', None, 'dp', None, 'spatial'), may hold values from -6 to 6
- fresh: bfloat16 [3, 4, 2, 256, 4, 128], P(None, None, 'dp', None, 'spatial'), may hold values from -6 to 6
- params: float32 [8, 2, 9, 256, 256], P('section', None, None, ('dp', 'spatial')), may hold values from -6 to 6
- moments: float32 [8, 2, 9, 256, 256], P('section', None, None, ('dp', 'spatial')), may hold values from -3 to 3
Outputs:
- outbox: bfloat16 [8, 4, 2, 256, 4, 128], P('section', None, 'dp', None, 'spatial')
- params_out: float32 [8, 2, 9, 256, 256], P('section', None, None, ('dp', 'spatial'))
- moments_out: float32 [8, 2, 9, 256, 256], P('section', None, None, ('dp', 'spatial'))
All inputs are finite; a program needn't handle non-finite values.
Results may differ from a plain program's by a relative error of at most 0.024.
Values may be sent and summed in bfloat16 or wider, within the bound.
No kernel may reach another device: no remote copies, remote signals or barrier semaphores. Data moves between devices by JAX's collectives and lax.ppermute only.
A program may use at most 64 MiB of HBM per device.

v0:
```python
import functools
import math

import jax
import jax.numpy as jnp
from jax import lax
from jax.experimental import pallas as pl
from jax.experimental.pallas import tpu as pltpu
from jax.sharding import PartitionSpec as P

learn_rate = 0.05
momentum_decay = 0.9

VMEM = pl.BlockSpec(memory_space=pltpu.VMEM)
SMEM = pl.BlockSpec(memory_space=pltpu.SMEM)
f32 = jnp.float32
bf16 = jnp.bfloat16


def ring(axis, shift):
    count = lax.axis_size(axis)
    return [((i + shift) % count, i) for i in range(count)]


def around(shard, axis):
    return [shard] + [
        lax.ppermute(shard, axis, ring(axis, k)) for k in range(1, lax.axis_size(axis))
    ]


def silu_slope(value):
    sigma = jax.nn.sigmoid(value)
    return sigma * (1.0 + value * (1.0 - sigma))


def silu16(value):
    value = value.astype(f32)
    return (value * jax.nn.sigmoid(value)).astype(bf16)


def lane_shift(value, by):
    width = value.shape[-1]
    moved = pltpu.roll(value, by % width, 1)
    lane = lax.broadcasted_iota(jnp.int32, value.shape, 1)
    edge = 0 if by > 0 else width - 1
    return jnp.where(lane == edge, jnp.zeros_like(moved), moved)


def conv_rows(load, count, kernel):
    stacked = jnp.concatenate(
        [jnp.concatenate([load(r + a) for r in range(count)], axis=1) for a in range(3)], axis=0
    )
    sums = [jnp.dot(kernel[b], stacked, preferred_element_type=f32) for b in range(3)]
    width = stacked.shape[1] // count
    rows = []
    for r in range(count):
        left, middle, right = (s[:, r * width : (r + 1) * width] for s in sums)
        rows.append(middle + lane_shift(left, 1) + lane_shift(right, -1))
    return rows


def stage_one(pieces, place, *refs):
    first, second = refs[:pieces], refs[pieces : 2 * pieces]
    kernel, flip, padded_a, padded_b, own, raw, other = refs[2 * pieces :]
    band = first[0].shape[1]
    rows = band * pieces
    zero = jnp.zeros(padded_a.shape[2:], bf16)
    for member in range(2):
        for edge in (0, rows + 1):
            padded_a[member, edge] = zero
            padded_b[member, edge] = zero
    me = place[0]
    for s in range(pieces):
        start = lax.rem(me + s, pieces) * band
        for r in range(band):
            half = first[s][0, r]
            raw[start + r] = half
            padded_a[0, start + r + 1] = silu16(half)
            padded_a[1, start + r + 1] = first[s][1, r]
            for member in range(2):
                other[member, start + r] = second[s][member, r]
    moved = conv_rows(lambda i: padded_a[0, i], rows, kernel)
    for r in range(rows):
        prev = (other[0, r].astype(f32) - moved[r]).astype(bf16)
        other[0, r] = prev
        padded_b[0, r + 1] = silu16(prev)
    moved = conv_rows(lambda i: padded_a[1, i], rows, flip)
    for r in range(rows):
        slope = silu_slope(raw[r].astype(f32))
        back = (other[1, r].astype(f32) + slope * moved[r]).astype(bf16)
        other[1, r] = back
        padded_b[1, r + 1] = back
    for member in range(2):
        for r in range(band):
            own[member, r] = other[member, me * band + r]


def stage_two(place, padded, first, second, kernel, flip, out):
    band = first.shape[1]
    base = place[0] * band
    moved = conv_rows(lambda i: padded[0, base + i], band, kernel)
    for r in range(band):
        out[0, r] = (first[0, r].astype(f32) - moved[r]).astype(bf16)
    moved = conv_rows(lambda i: padded[1, base + i], band, flip)
    for r in range(band):
        slope = silu_slope(second[0, r].astype(f32))
        out[1, r] = (first[1, r].astype(f32) + slope * moved[r]).astype(bf16)


def update(pieces, images, final, scale, place, padded, *refs):
    count = pieces * (images - 1)
    given, refs = refs[:count], refs[count:]
    if final:
        params, moments, params_out, moments_out, act, cot, moved = refs
    else:
        (weights, speed, params, moments, weights_out, flip_out, speed_out, params_out,
         moments_out, act, cot, moved, total) = refs
    me, mine = place[0], place[1]
    rows = padded.shape[1] - 2
    band = rows // pieces
    channels = padded.shape[2]
    part = params.shape[1]
    for r in range(rows):
        act[r] = padded[0, r + 1]
        cot[r] = padded[1, r + 1]
    for image in range(images - 1):
        for s in range(pieces):
            piece = given[image * pieces + s]
            start = (image + 1) * rows + lax.rem(me + s, pieces) * band
            for r in range(band):
                act[start + r] = silu16(piece[0, r])
                cot[start + r] = piece[1, r]
    slot = pl.ds(pl.multiple_of(mine * part, part), part)
    for b in range(3):
        source = cot
        if b != 1:
            source = moved
            for r in range(images * rows):
                moved[r] = lane_shift(cot[r].astype(f32), b - 1).astype(bf16)
        for a in range(3):
            valid = [
                (i * rows + r, i * rows + r + a - 1)
                for i in range(images)
                for r in range(rows)
                if 0 <= r + a - 1 < rows
            ]
            if final:
                left = jnp.concatenate([source[r, slot, :] for r, _ in valid], axis=1)
            else:
                left = jnp.concatenate([source[r] for r, _ in valid], axis=1)
            right = jnp.concatenate([act[r] for _, r in valid], axis=1)
            grad = lax.dot_general(
                left, right, (((1,), (1,)), ((), ())), preferred_element_type=f32
            )
            tap = 3 * a + b
            if final:
                mine_grad = grad
            else:
                total[...] = grad
                mine_grad = total[slot, :]
            step = momentum_decay * moments[tap] + scale * mine_grad
            moments_out[tap] = step
            params_out[tap] = params[tap] - learn_rate * step
            if not final:
                cols = slice(a * channels, (a + 1) * channels)
                step = momentum_decay * speed[b, :, cols].astype(f32) + scale * grad
                speed_out[b, :, cols] = step.astype(bf16)
                fresh = weights[b, :, cols].astype(f32) - (learn_rate * scale) * step
                weights_out[b, :, cols] = fresh.astype(bf16)
                back = slice((2 - a) * channels, (3 - a) * channels)
                flip_out[2 - b, :, back] = fresh.T.astype(bf16)


def assemble(sections, pieces, flipping, place, *refs):
    count = sections * pieces
    given = refs[:count]
    out = refs[count]
    part, channels = given[0].shape[1:]
    me, at = place[0], place[2]
    for d in range(sections):
        for s in range(pieces):
            owner = lax.rem(at + d, sections) * pieces + lax.rem(me + s, pieces)
            slot = pl.ds(pl.multiple_of(owner * part, part), part)
            for a in range(3):
                for b in range(3):
                    out[b, slot, a * channels : (a + 1) * channels] = given[d * pieces + s][3 * a + b]
    if flipping:
        flip = refs[count + 1]
        for a in range(3):
            for b in range(3):
                block = out[b, :, a * channels : (a + 1) * channels].astype(f32)
                flip[2 - b, :, (2 - a) * channels : (3 - a) * channels] = block.T.astype(bf16)


def call(body, outs, inputs, flops, scratch=()):
    size = sum(math.prod(x.shape) * x.dtype.itemsize for x in list(inputs) + list(outs))
    return pl.pallas_call(
        body,
        out_shape=outs,
        in_specs=[SMEM] + [VMEM] * (len(inputs) - 1),
        out_specs=[VMEM] * len(outs),
        scratch_shapes=list(scratch),
        compiler_params=pltpu.CompilerParams(vmem_limit_bytes=32 * 1024 * 1024),
        cost_estimate=pl.CostEstimate(flops=flops, bytes_accessed=size, transcendentals=0),
    )(*inputs)


def local(inbox, fresh, params, moments):
    channels, band, width = inbox.shape[3:]
    scale = 1.0 / math.sqrt(9 * channels)
    pieces = lax.axis_size("spatial")
    images = lax.axis_size("dp")
    rows = band * pieces
    ticks = fresh.shape[0] + 1
    sections = lax.axis_size("section")
    top_section = lax.axis_index("section") == sections - 1
    me, at = lax.axis_index("spatial"), lax.axis_index("dp")
    place = jnp.stack([me, at * pieces + me, at]).astype(jnp.int32)
    shape = functools.partial(jax.ShapeDtypeStruct)
    message = shape((2, band, channels, width), bf16)
    padded = shape((2, rows + 2, channels, width), bf16)
    block = shape((3, channels, 3 * channels), bf16)
    conv_flops = 2 * 2 * 9 * channels * channels * rows * width
    share = params.shape[3]

    def rowwise(stack, members):
        return jnp.stack([jnp.swapaxes(stack[m, 0], 0, 1) for m in members])

    def gathered(shard, flipping):
        parts = [q for p in around(shard, "dp") for q in around(p, "spatial")]
        body = functools.partial(assemble, images, pieces, flipping)
        return call(body, [block] * (2 if flipping else 1), [place] + parts, channels**3)

    def one(first, second, kernel, flip):
        inputs = [place] + around(first, "spatial") + second + [kernel, flip]
        scratch = [pltpu.VMEM((rows, channels, width), bf16), pltpu.VMEM((2, rows, channels, width), bf16)]
        return call(
            functools.partial(stage_one, pieces), [padded, padded, message], inputs, conv_flops, scratch
        )

    def two(padded_b, first, second, kernel, flip):
        inputs = [place, padded_b, first, second, kernel, flip]
        return call(stage_two, [message], inputs, conv_flops // pieces)[0]

    def abroad(shard):
        return [q for p in around(shard, "dp")[1:] for q in around(p, "spatial")]

    def learn(padded_own, others, state, final):
        weights, speed, own_params, own_moments = state
        own = shape(own_params.shape, f32)
        field = pltpu.VMEM((images * rows, channels, width), bf16)
        scratch = [field] * 3
        outs = [own, own]
        inputs = [place, padded_own] + others
        if final:
            inputs += [own_params, own_moments]
        else:
            inputs += [weights, speed, own_params, own_moments]
            outs = [block] * 3 + outs
            scratch += [pltpu.VMEM((channels, channels), f32)]
        body = functools.partial(update, pieces, images, final, scale)
        flops = 2 * 9 * channels * channels * rows * width * images
        return call(body, outs, inputs, flops, scratch)

    first = rowwise(inbox[0], (0, 3))
    second = rowwise(inbox[0], (1, 2))
    kernels = (params[0] * scale).astype(bf16)
    speeds = moments[0].astype(bf16)
    weights_g, flip_g = gathered(kernels[1], True)
    weights_f, flip_f = gathered(kernels[0], True)
    (speed_g,) = gathered(speeds[1], False)
    (speed_f,) = gathered(speeds[0], False)
    params_f, params_g = params[0, 0], params[0, 1]
    moments_f, moments_g = moments[0, 0], moments[0, 1]
    down = [(i, i - 1) for i in range(1, sections)]
    second_all = around(second, "spatial")
    for tick in range(ticks):
        final = tick == ticks - 1
        padded_a, padded_b, middle = one(first, second_all, weights_g, flip_g)
        if not final:
            second = jnp.where(
                top_section, rowwise(fresh[tick], (1, 2)), lax.ppermute(middle, "section", down)
            )
            second_all = around(second, "spatial")
        last = two(padded_b, first, middle, weights_f, flip_f)
        others_g = abroad(first)
        others_f = abroad(middle)
        if not final:
            first = jnp.where(
                top_section, rowwise(fresh[tick], (0, 3)), lax.ppermute(last, "section", down)
            )
        state_g = (weights_g, speed_g, params_g, moments_g)
        state_f = (weights_f, speed_f, params_f, moments_f)
        if final:
            params_g, moments_g = learn(padded_a, others_g, state_g, True)
            params_f, moments_f = learn(padded_b, others_f, state_f, True)
        else:
            weights_g, flip_g, speed_g, params_g, moments_g = learn(padded_a, others_g, state_g, False)
            weights_f, flip_f, speed_f, params_f, moments_f = learn(padded_b, others_f, state_f, False)
    sent = jnp.stack([last[0], middle[0], middle[1], last[1]])
    outbox = jnp.swapaxes(sent, 1, 2)[None, :, None]
    return (
        outbox,
        jnp.stack([params_f, params_g])[None],
        jnp.stack([moments_f, moments_g])[None],
    )


def solution(mesh):
    placed = (
        P("section", None, "dp", None, "spatial", None),
        P(None, None, "dp", None, "spatial", None),
        P("section", None, None, ("dp", "spatial"), None),
        P("section", None, None, ("dp", "spatial"), None),
    )
    return jax.shard_map(
        local,
        mesh=mesh,
        in_specs=placed,
        out_specs=(
            P("section", None, "dp", None, "spatial", None),
            P("section", None, None, ("dp", "spatial"), None),
            P("section", None, None, ("dp", "spatial"), None),
        ),
        check_vma=False,
    )
```

profile of v0, /device:TPU:21, one launch (start us, length us, event | category | flops | bytes accessed | tf_op | source)
XLA Modules:
  0.0 137.6 jit_solution(2042298938342560945)
XLA Ops:
  8.1 3.3 %collective-permute-done.3.refs_2_ = bf16[9,64,256]{2,1,0:T(8,128)(2,1)S(1)} collective-permute-done((bf16[9,64,256]{2,1,0:T(8,128)(2,1)S(1)}, bf16[9,64,256]{2,1,0:T(8,128)(2,1)S(1)}, u32[]{:S(2)}, u32[]{:S(2)}) %collective-permute-start.3) | collective-permute-done | bytes 294944 | tf_op jit(solution)/shard_map/ppermute | solution.py:27
  12.9 4.8 %collective-permute-done.6.refs_2_ = bf16[9,64,256]{2,1,0:T(8,128)(2,1)S(1)} collective-permute-done((bf16[9,64,256]{2,1,0:T(8,128)(2,1)S(1)}, bf16[9,64,256]{2,1,0:T(8,128)(2,1)S(1)}, u32[]{:S(2)}, u32[]{:S(2)}) %collective-permute-start.6) | collective-permute-done | bytes 294944 | tf_op jit(solution)/shard_map/ppermute | solution.py:27
  18.8 3.5 %fusion = (bf16[1,1,1,256,2,128]{5,4,3,2,1,0:T(2,128)(2,1)}, bf16[1,1,1,256,2,128]{5,4,3,2,1,0:T(2,128)(2,1)}, bf16[1,1,1,256,2,128]{5,4,3,2,1,0:T(2,128)(2,1)},...) fusion(bf16[3,4,1,256,2,128]{5,4,3,2,1,0:T(2,128)(2,1)} %param.5), kind=kLoop, calls=%fused_computation.37 | loop fusion | bytes 3145728 | tf_op jit(solution)/shard_map/slice | solution.py:227
  28.8 3.8 %shard_map.68 = (bf16[2,6,256,128]{3,2,1,0:T(8,128)(2,1)S(1)}, bf16[2,6,256,128]{3,2,1,0:T(8,128)(2,1)S(1)}, bf16[2,2,256,128]{3,2,1,0:T(8,128)(2,1)}) custom-call(s32[3]{0:T(128)S(1)} %pad_add_fusion.place, bf16[2,2,256,128]{3,2,1,0:T(8,128)(2,1)} %pad_maximum_fusion.refs_0_.first, bf16[2,2,256,128]{3,2,1,0:T(8,128)(2,1)} %collective-permute-done.refs_1_, ...), custom_call_target="tpu_custom_call" | custom-call | flops 1207959552 | bytes 5242892 | tf_op jit(solution)/shard_map/pallas_call | solution.py:197
  33.5 2.6 %shard_map.70 = bf16[2,2,256,128]{3,2,1,0:T(8,128)(2,1)} custom-call(s32[3]{0:T(128)S(1)} %pad_add_fusion.place, bf16[2,6,256,128]{3,2,1,0:T(8,128)(2,1)S(1)} %get-tuple-element.53.padded, bf16[2,2,256,128]{3,2,1,0:T(8,128)(2,1)} %pad_maximum_fusion.refs_0_.first, bf16[2,2,256,128]{3,2,1,0:T(8,128)(2,1)} %get-tuple-element.54.second, ...), custom_call_target="tpu_custom_call" | custom-call | flops 603979776 | bytes 3932172 | tf_op jit(solution)/shard_map/pallas_call | solution.py:197
  36.1 2.1 %collective-permute-start.8 = (bf16[2,2,256,128]{3,2,1,0:T(8,128)(2,1)}, bf16[2,2,256,128]{3,2,1,0:T(8,128)(2,1)}, u32[]{:S(2)}, u32[]{:S(2)}) collective-permute-start(bf16[2,2,256,128]{3,2,1,0:T(8,128)(2,1)} %shard_map.70), channel_id=1, source_target_pairs={{4,0},{8,4},{12,8},{16,12},{20,16},{24,20},{28,24},{5,1},{9,5},{13... | collective-permute-start | bytes 786440 | tf_op jit(solution)/shard_map/ppermute | solution.py:290
  39.0 3.2 %collective-permute-start.10 = (bf16[2,2,256,128]{3,2,1,0:T(8,128)(2,1)}, bf16[2,2,256,128]{3,2,1,0:T(8,128)(2,1)}, u32[]{:S(2)}, u32[]{:S(2)}) collective-permute-start(bf16[2,2,256,128]{3,2,1,0:T(8,128)(2,1)} %get-tuple-element.54.second), channel_id=1, source_target_pairs={{4,0},{8,4},{12,8},{16,12},{20,16},{24,20},{28,24},{5,1},{9,5},{13... | collective-permute-start | bytes 786440 | tf_op jit(solution)/shard_map/ppermute | solution.py:282
  43.0 1.9 %collective-permute-start.14 = (bf16[9,64,256]{2,1,0:T(8,128)(2,1)}, bf16[9,64,256]{2,1,0:T(8,128)(2,1)S(1)}, u32[]{:S(2)}, u32[]{:S(2)}) collective-permute-start(bf16[9,64,256]{2,1,0:T(8,128)(2,1)} %get-tuple-element.119.refs_0_), channel_id=1, source_target_pairs={{1,0},{0,1},{3,2},{2,3},{5,4},{4,5},{7,6},{6,7},{9,8},{8,9},{11,10... | collective-permute-start | bytes 884744 | tf_op jit(solution)/shard_map/ppermute | solution.py:27
  47.1 4.3 %collective-permute-done.10 = bf16[2,2,256,128]{3,2,1,0:T(8,128)(2,1)} collective-permute-done((bf16[2,2,256,128]{3,2,1,0:T(8,128)(2,1)}, bf16[2,2,256,128]{3,2,1,0:T(8,128)(2,1)}, u32[]{:S(2)}, u32[]{:S(2)}) %collective-permute-start.10) | collective-permute-done | bytes 262176 | tf_op jit(solution)/shard_map/ppermute | solution.py:282
  51.4 2.2 %collective-permute-start.21 = (bf16[9,64,256]{2,1,0:T(8,128)(2,1)}, bf16[9,64,256]{2,1,0:T(8,128)(2,1)S(1)}, u32[]{:S(2)}, u32[]{:S(2)}) collective-permute-start(bf16[9,64,256]{2,1,0:T(8,128)(2,1)} %collective-permute-done.20.refs_2_), channel_id=1, source_target_pairs={{1,0},{0,1},{3,2},{2,3},{5,4},{4,5},{7,6},{6,7},{9,8},{8,9},{11,10... | collective-permute-start | bytes 884744 | tf_op jit(solution)/shard_map/ppermute | solution.py:27
  59.2 2.9 %shard_map.72 = (bf16[3,256,768]{2,1,0:T(8,128)(2,1)S(1)}, bf16[3,256,768]{2,1,0:T(8,128)(2,1)S(1)}, bf16[3,256,768]{2,1,0:T(8,128)(2,1)S(1)}, f32[9,64,256]{2,1,0:T(8,128)S(1)}, f32[9,64,256]{2,1,0:T(8,128)S(1)}) custom-call(s32[3]{0:T(128)S(1)} %pad_add_fusion.place, bf16[2,6,256,128]{3,2,1,0:T(8,128)(2,1)S(1)} %copy-done.3, ...), custom_call_target="tpu_custom_call" | custom-call | flops 1207959552 | bytes 9568268 | tf_op jit(solution)/shard_map/pallas_call | solution.py:197
  62.4 2.6 %shard_map.73 = (bf16[2,6,256,128]{3,2,1,0:T(8,128)(2,1)S(1)}, bf16[2,6,256,128]{3,2,1,0:T(8,128)(2,1)S(1)}, bf16[2,2,256,128]{3,2,1,0:T(8,128)(2,1)S(1)}) custom-call(s32[3]{0:T(128)S(1)} %pad_add_fusion.place, bf16[2,2,256,128]{3,2,1,0:T(8,128)(2,1)S(1)} %maximum_select_fusion.2.refs_0_.first, bf16[2,2,256,128]{3,2,1,0:T(8,128)(2,1)S(1)} %collective-permute-done.9.refs_1_, ...), custom_call_target="tpu_custom_call" | custom-call | flops 1207959552 | bytes 5242892 | tf_op jit(solution)/shard_map/pallas_call | solution.py:197
  65.0 2.6 %shard_map.75 = (bf16[3,256,768]{2,1,0:T(8,128)(2,1)S(1)}, bf16[3,256,768]{2,1,0:T(8,128)(2,1)S(1)}, bf16[3,256,768]{2,1,0:T(8,128)(2,1)S(1)}, f32[9,64,256]{2,1,0:T(8,128)S(1)}, f32[9,64,256]{2,1,0:T(8,128)S(1)}) custom-call(s32[3]{0:T(128)S(1)} %pad_add_fusion.place, bf16[2,6,256,128]{3,2,1,0:T(8,128)(2,1)S(1)} %get-tuple-element.53.padded, ...), custom_call_target="tpu_custom_call" | custom-call | flops 1207959552 | bytes 9568268 | tf_op jit(solution)/shard_map/pallas_call | solution.py:197
  69.1 1.9 %collective-permute-start.22 = (bf16[2,2,256,128]{3,2,1,0:T(8,128)(2,1)S(1)}, bf16[2,2,256,128]{3,2,1,0:T(8,128)(2,1)S(1)}, u32[]{:S(2)}, u32[]{:S(2)}) collective-permute-start(bf16[2,2,256,128]{3,2,1,0:T(8,128)(2,1)S(1)} %shard_map.76), channel_id=1, source_target_pairs={{4,0},{8,4},{12,8},{16,12},{20,16},{24,20},{28,24},{5,1},{9,5},{13... | collective-permute-start | bytes 786440 | tf_op jit(solution)/shard_map/ppermute | solution.py:290
  71.1 3.5 %collective-permute-start.24 = (bf16[2,2,256,128]{3,2,1,0:T(8,128)(2,1)S(1)}, bf16[2,2,256,128]{3,2,1,0:T(8,128)(2,1)S(1)}, u32[]{:S(2)}, u32[]{:S(2)}) collective-permute-start(bf16[2,2,256,128]{3,2,1,0:T(8,128)(2,1)S(1)} %get-tuple-element.61.second), channel_id=1, source_target_pairs={{4,0},{8,4},{12,8},{16,12},{20,16},{24,20},{28,24},{5,1},{9,5},{13... | collective-permute-start | bytes 786440 | tf_op jit(solution)/shard_map/ppermute | solution.py:282
  77.0 2.5 %collective-permute-done.22 = bf16[2,2,256,128]{3,2,1,0:T(8,128)(2,1)S(1)} collective-permute-done((bf16[2,2,256,128]{3,2,1,0:T(8,128)(2,1)S(1)}, bf16[2,2,256,128]{3,2,1,0:T(8,128)(2,1)S(1)}, u32[]{:S(2)}, u32[]{:S(2)}) %collective-permute-start.22) | collective-permute-done | bytes 262176 | tf_op jit(solution)/shard_map/ppermute | solution.py:290
  79.5 1.9 %collective-permute-start.23 = (bf16[2,2,256,128]{3,2,1,0:T(8,128)(2,1)S(1)}, bf16[2,2,256,128]{3,2,1,0:T(8,128)(2,1)S(1)}, u32[]{:S(2)}, u32[]{:S(2)}) collective-permute-start(bf16[2,2,256,128]{3,2,1,0:T(8,128)(2,1)S(1)} %maximum_select_fusion.1.refs_0_.first), channel_id=1, source_target_pairs={{1,0},{0,1},{3,2},{2,3},{5,4},{4,5},{7,6},{6,7},{9,8},{8,9},{11,10... | collective-permute-start | bytes 786440 | tf_op jit(solution)/shard_map/ppermute | solution.py:27
  81.4 3.7 %collective-permute-done.24 = bf16[2,2,256,128]{3,2,1,0:T(8,128)(2,1)S(1)} collective-permute-done((bf16[2,2,256,128]{3,2,1,0:T(8,128)(2,1)S(1)}, bf16[2,2,256,128]{3,2,1,0:T(8,128)(2,1)S(1)}, u32[]{:S(2)}, u32[]{:S(2)}) %collective-permute-start.24) | collective-permute-done | bytes 262176 | tf_op jit(solution)/shard_map/ppermute | solution.py:282
  87.6 2.5 %shard_map.77 = (bf16[3,256,768]{2,1,0:T(8,128)(2,1)S(1)}, bf16[3,256,768]{2,1,0:T(8,128)(2,1)S(1)}, bf16[3,256,768]{2,1,0:T(8,128)(2,1)S(1)}, f32[9,64,256]{2,1,0:T(8,128)S(1)}, f32[9,64,256]{2,1,0:T(8,128)S(1)}) custom-call(s32[3]{0:T(128)S(1)} %pad_add_fusion.place, bf16[2,6,256,128]{3,2,1,0:T(8,128)(2,1)S(1)} %get-tuple-element.64.padded, ...), custom_call_target="tpu_custom_call" | custom-call | flops 1207959552 | bytes 9568268 | tf_op jit(solution)/shard_map/pallas_call | solution.py:197
  90.2 2.6 %shard_map.78 = (bf16[2,6,256,128]{3,2,1,0:T(8,128)(2,1)S(1)}, bf16[2,6,256,128]{3,2,1,0:T(8,128)(2,1)S(1)}, bf16[2,2,256,128]{3,2,1,0:T(8,128)(2,1)S(1)}) custom-call(s32[3]{0:T(128)S(1)} %pad_add_fusion.place, bf16[2,2,256,128]{3,2,1,0:T(8,128)(2,1)S(1)} %maximum_select_fusion.1.refs_0_.first, ...), custom_call_target="tpu_custom_call" | custom-call | flops 1207959552 | bytes 5242892 | tf_op jit(solution)/shard_map/pallas_call | solution.py:197
  92.8 2.6 %shard_map.79 = (bf16[3,256,768]{2,1,0:T(8,128)(2,1)S(1)}, bf16[3,256,768]{2,1,0:T(8,128)(2,1)S(1)}, bf16[3,256,768]{2,1,0:T(8,128)(2,1)S(1)}, f32[9,64,256]{2,1,0:T(8,128)S(1)}, f32[9,64,256]{2,1,0:T(8,128)S(1)}) custom-call(s32[3]{0:T(128)S(1)} %pad_add_fusion.place, bf16[2,6,256,128]{3,2,1,0:T(8,128)(2,1)S(1)} %get-tuple-element.60.padded, ...), custom_call_target="tpu_custom_call" | custom-call | flops 1207959552 | bytes 9568268 | tf_op jit(solution)/shard_map/pallas_call | solution.py:197
  96.8 1.9 %collective-permute-start.30 = (bf16[2,2,256,128]{3,2,1,0:T(8,128)(2,1)S(1)}, bf16[2,2,256,128]{3,2,1,0:T(8,128)(2,1)S(1)}, u32[]{:S(2)}, u32[]{:S(2)}) collective-permute-start(bf16[2,2,256,128]{3,2,1,0:T(8,128)(2,1)S(1)} %shard_map.80), channel_id=1, source_target_pairs={{4,0},{8,4},{12,8},{16,12},{20,16},{24,20},{28,24},{5,1},{9,5},{13... | collective-permute-start | bytes 786440 | tf_op jit(solution)/shard_map/ppermute | solution.py:290
  98.8 3.5 %collective-permute-start.32 = (bf16[2,2,256,128]{3,2,1,0:T(8,128)(2,1)S(1)}, bf16[2,2,256,128]{3,2,1,0:T(8,128)(2,1)S(1)}, u32[]{:S(2)}, u32[]{:S(2)}) collective-permute-start(bf16[2,2,256,128]{3,2,1,0:T(8,128)(2,1)S(1)} %get-tuple-element.71.second), channel_id=1, source_target_pairs={{4,0},{8,4},{12,8},{16,12},{20,16},{24,20},{28,24},{5,1},{9,5},{13... | collective-permute-start | bytes 786440 | tf_op jit(solution)/shard_map/ppermute | solution.py:282
  104.2 2.5 %collective-permute-done.30 = bf16[2,2,256,128]{3,2,1,0:T(8,128)(2,1)S(1)} collective-permute-done((bf16[2,2,256,128]{3,2,1,0:T(8,128)(2,1)S(1)}, bf16[2,2,256,128]{3,2,1,0:T(8,128)(2,1)S(1)}, u32[]{:S(2)}, u32[]{:S(2)}) %collective-permute-start.30) | collective-permute-done | bytes 262176 | tf_op jit(solution)/shard_map/ppermute | solution.py:290
  106.8 2.8 %collective-permute-start.31 = (bf16[2,2,256,128]{3,2,1,0:T(8,128)(2,1)S(1)}, bf16[2,2,256,128]{3,2,1,0:T(8,128)(2,1)S(1)}, u32[]{:S(2)}, u32[]{:S(2)}) collective-permute-start(bf16[2,2,256,128]{3,2,1,0:T(8,128)(2,1)S(1)} %maximum_select_fusion.refs_0_.first), channel_id=1, source_target_pairs={{1,0},{0,1},{3,2},{2,3},{5,4},{4,5},{7,6},{6,7},{9,8},{8,9},{11,10... | collective-permute-start | bytes 786440 | tf_op jit(solution)/shard_map/ppermute | solution.py:27
  109.6 2.8 %collective-permute-done.32 = bf16[2,2,256,128]{3,2,1,0:T(8,128)(2,1)S(1)} collective-permute-done((bf16[2,2,256,128]{3,2,1,0:T(8,128)(2,1)S(1)}, bf16[2,2,256,128]{3,2,1,0:T(8,128)(2,1)S(1)}, u32[]{:S(2)}, u32[]{:S(2)}) %collective-permute-start.32) | collective-permute-done | bytes 262176 | tf_op jit(solution)/shard_map/ppermute | solution.py:282
  112.4 1.6 %collective-permute-start.33 = (bf16[2,2,256,128]{3,2,1,0:T(8,128)(2,1)S(1)}, bf16[2,2,256,128]{3,2,1,0:T(8,128)(2,1)S(1)}, u32[]{:S(2)}, u32[]{:S(2)}) collective-permute-start(bf16[2,2,256,128]{3,2,1,0:T(8,128)(2,1)S(1)} %maximum_select_fusion.5.refs_2_), channel_id=1, source_target_pairs={{1,0},{0,1},{3,2},{2,3},{5,4},{4,5},{7,6},{6,7},{9,8},{8,9},{11,10... | collective-permute-start | bytes 786440 | tf_op jit(solution)/shard_map/ppermute | solution.py:27
  114.7 3.5 %shard_map.81 = (bf16[3,256,768]{2,1,0:T(8,128)(2,1)S(1)}, bf16[3,256,768]{2,1,0:T(8,128)(2,1)S(1)}, bf16[3,256,768]{2,1,0:T(8,128)(2,1)}, f32[9,64,256]{2,1,0:T(8,128)S(1)}, f32[9,64,256]{2,1,0:T(8,128)S(1)}) custom-call(s32[3]{0:T(128)S(1)} %pad_add_fusion.place, bf16[2,6,256,128]{3,2,1,0:T(8,128)(2,1)S(1)} %get-tuple-element.77.padded, ...), custom_call_target="tpu_custom_call" | custom-call | flops 1207959552 | bytes 9568268 | tf_op jit(solution)/shard_map/pallas_call | solution.py:197
  118.2 2.6 %shard_map.82 = (bf16[2,6,256,128]{3,2,1,0:T(8,128)(2,1)S(1)}, bf16[2,6,256,128]{3,2,1,0:T(8,128)(2,1)S(1)}, bf16[2,2,256,128]{3,2,1,0:T(8,128)(2,1)S(1)}) custom-call(s32[3]{0:T(128)S(1)} %pad_add_fusion.place, bf16[2,2,256,128]{3,2,1,0:T(8,128)(2,1)S(1)} %maximum_select_fusion.refs_0_.first, bf16[2,2,256,128]{3,2,1,0:T(8,128)(2,1)S(1)} %collective-permute-done.31.refs_1_, ...), custom_call_target="tpu_custom_call" | custom-call | flops 1207959552 | bytes 5242892 | tf_op jit(solution)/shard_map/pallas_call | solution.py:197
  122.8 3.5 %shard_map.83 = (bf16[3,256,768]{2,1,0:T(8,128)(2,1)S(1)}, bf16[3,256,768]{2,1,0:T(8,128)(2,1)S(1)}, bf16[3,256,768]{2,1,0:T(8,128)(2,1)}, f32[9,64,256]{2,1,0:T(8,128)S(1)}, f32[9,64,256]{2,1,0:T(8,128)S(1)}) custom-call(s32[3]{0:T(128)S(1)} %pad_add_fusion.place, bf16[2,6,256,128]{3,2,1,0:T(8,128)(2,1)S(1)} %get-tuple-element.70.padded, ...), custom_call_target="tpu_custom_call" | custom-call | flops 1207959552 | bytes 9568268 | tf_op jit(solution)/shard_map/pallas_call | solution.py:197
  131.0 2.2 %shard_map.86 = (f32[9,64,256]{2,1,0:T(8,128)S(1)}, f32[9,64,256]{2,1,0:T(8,128)S(1)}) custom-call(s32[3]{0:T(128)S(1)} %pad_add_fusion.place, bf16[2,6,256,128]{3,2,1,0:T(8,128)(2,1)S(1)} %get-tuple-element.93.padded, bf16[2,2,256,128]{3,2,1,0:T(8,128)(2,1)S(1)} %collective-permute-done.40.refs_0_, ...), custom_call_target="tpu_custom_call" | custom-call | flops 1207959552 | bytes 3670028 | tf_op jit(solution)/shard_map/pallas_call | solution.py:197
  133.2 2.2 %shard_map.85 = (f32[9,64,256]{2,1,0:T(8,128)S(1)}, f32[9,64,256]{2,1,0:T(8,128)S(1)}) custom-call(s32[3]{0:T(128)S(1)} %pad_add_fusion.place, bf16[2,6,256,128]{3,2,1,0:T(8,128)(2,1)S(1)} %get-tuple-element.83.padded, bf16[2,2,256,128]{3,2,1,0:T(8,128)(2,1)S(1)} %collective-permute-done.38.refs_0_, ...), custom_call_target="tpu_custom_call" | custom-call | flops 1207959552 | bytes 3670028 | tf_op jit(solution)/shard_map/pallas_call | solution.py:197
  (142 shorter events, 46.4 us)
Async XLA Ops:
  2.2 16.6 %collective-permute-start.2 = (bf16[9,64,256]{2,1,0:T(8,128)(2,1)S(1)}, bf16[9,64,256]{2,1,0:T(8,128)(2,1)S(1)}, u32[]{:S(2)}, u32[]{:S(2)}) collective-permute-start(bf16[9,64,256]{2,1,0:T(8,128)(2,1)S(1)} %get-tuple-element.121.refs_0_), channel_id=1, source_target_pairs={{1,0},{0,1},{3,2},{2,3},{5,4},{4,5},{7,6},{6,7},{9,8},{8,9},{11,10... | collective-permute-start | bytes 884744 | tf_op jit(solution)/shard_map/ppermute | solution.py:27
  2.9 8.5 %collective-permute-start.3 = (bf16[9,64,256]{2,1,0:T(8,128)(2,1)S(1)}, bf16[9,64,256]{2,1,0:T(8,128)(2,1)S(1)}, u32[]{:S(2)}, u32[]{:S(2)}) collective-permute-start(bf16[9,64,256]{2,1,0:T(8,128)(2,1)S(1)} %get-tuple-element.121.refs_0_), channel_id=1, source_target_pairs={{2,0},{0,2},{3,1},{1,3},{6,4},{4,6},{7,5},{5,7},{10,8},{8,10},{11,... | collective-permute-start | bytes 884744 | tf_op jit(solution)/shard_map/ppermute | solution.py:27
  4.1 20.5 %collective-permute-start.5 = (bf16[9,64,256]{2,1,0:T(8,128)(2,1)S(1)}, bf16[9,64,256]{2,1,0:T(8,128)(2,1)S(1)}, u32[]{:S(2)}, u32[]{:S(2)}) collective-permute-start(bf16[9,64,256]{2,1,0:T(8,128)(2,1)S(1)} %get-tuple-element.120.refs_0_), channel_id=1, source_target_pairs={{1,0},{0,1},{3,2},{2,3},{5,4},{4,5},{7,6},{6,7},{9,8},{8,9},{11,10... | collective-permute-start | bytes 884744 | tf_op jit(solution)/shard_map/ppermute | solution.py:27
  4.5 13.2 %collective-permute-start.6 = (bf16[9,64,256]{2,1,0:T(8,128)(2,1)S(1)}, bf16[9,64,256]{2,1,0:T(8,128)(2,1)S(1)}, u32[]{:S(2)}, u32[]{:S(2)}) collective-permute-start(bf16[9,64,256]{2,1,0:T(8,128)(2,1)S(1)} %get-tuple-element.120.refs_0_), channel_id=1, source_target_pairs={{2,0},{0,2},{3,1},{1,3},{6,4},{4,6},{7,5},{5,7},{10,8},{8,10},{11,... | collective-permute-start | bytes 884744 | tf_op jit(solution)/shard_map/ppermute | solution.py:27
  5.9 22.9 %collective-permute-start = (bf16[2,2,256,128]{3,2,1,0:T(8,128)(2,1)}, bf16[2,2,256,128]{3,2,1,0:T(8,128)(2,1)}, u32[]{:S(2)}, u32[]{:S(2)}) collective-permute-start(bf16[2,2,256,128]{3,2,1,0:T(8,128)(2,1)} %pad_maximum_fusion.refs_0_.first), channel_id=1, source_target_pairs={{1,0},{0,1},{3,2},{2,3},{5,4},{4,5},{7,6},{6,7},{9,8},{8,9},{11,10... | collective-permute-start | bytes 786440 | tf_op jit(solution)/shard_map/ppermute | solution.py:27
  11.4 10.8 %collective-permute-start.4 = (bf16[9,64,256]{2,1,0:T(8,128)(2,1)S(1)}, bf16[9,64,256]{2,1,0:T(8,128)(2,1)S(1)}, u32[]{:S(2)}, u32[]{:S(2)}) collective-permute-start(bf16[9,64,256]{2,1,0:T(8,128)(2,1)S(1)} %collective-permute-done.3.refs_2_), channel_id=1, source_target_pairs={{1,0},{0,1},{3,2},{2,3},{5,4},{4,5},{7,6},{6,7},{9,8},{8,9},{11,10... | collective-permute-start | bytes 884744 | tf_op jit(solution)/shard_map/ppermute | solution.py:27
  18.7 10.1 %collective-permute-start.1 = (bf16[2,2,256,128]{3,2,1,0:T(8,128)(2,1)S(1)}, bf16[2,2,256,128]{3,2,1,0:T(8,128)(2,1)S(1)}, u32[]{:S(2)}, u32[]{:S(2)}) collective-permute-start(bf16[2,2,256,128]{3,2,1,0:T(8,128)(2,1)S(1)} %pad_maximum_fusion.1.refs_2_), channel_id=1, source_target_pairs={{1,0},{0,1},{3,2},{2,3},{5,4},{4,5},{7,6},{6,7},{9,8},{8,9},{11,10... | collective-permute-start | bytes 786440 | tf_op jit(solution)/shard_map/ppermute | solution.py:27
  22.2 20.7 %collective-permute-start.12 = (bf16[2,2,256,128]{3,2,1,0:T(8,128)(2,1)}, bf16[2,2,256,128]{3,2,1,0:T(8,128)(2,1)}, u32[]{:S(2)}, u32[]{:S(2)}) collective-permute-start(bf16[2,2,256,128]{3,2,1,0:T(8,128)(2,1)} %pad_maximum_fusion.refs_0_.first), channel_id=1, source_target_pairs={{2,0},{0,2},{3,1},{1,3},{6,4},{4,6},{7,5},{5,7},{10,8},{8,10},{11,... | collective-permute-start | bytes 786440 | tf_op jit(solution)/shard_map/ppermute | solution.py:27
  25.3 19.5 %collective-permute-start.15 = (bf16[9,64,256]{2,1,0:T(8,128)(2,1)}, bf16[9,64,256]{2,1,0:T(8,128)(2,1)}, u32[]{:S(2)}, u32[]{:S(2)}) collective-permute-start(bf16[9,64,256]{2,1,0:T(8,128)(2,1)} %get-tuple-element.119.refs_0_), channel_id=1, source_target_pairs={{2,0},{0,2},{3,1},{1,3},{6,4},{4,6},{7,5},{5,7},{10,8},{8,10},{11,... | collective-permute-start | bytes 884744 | tf_op jit(solution)/shard_map/ppermute | solution.py:27
  25.6 19.4 %collective-permute-start.20 = (bf16[9,64,256]{2,1,0:T(8,128)(2,1)S(1)}, bf16[9,64,256]{2,1,0:T(8,128)(2,1)}, u32[]{:S(2)}, u32[]{:S(2)}) collective-permute-start(bf16[9,64,256]{2,1,0:T(8,128)(2,1)S(1)} %get-tuple-element.118.refs_0_), channel_id=1, source_target_pairs={{2,0},{0,2},{3,1},{1,3},{6,4},{4,6},{7,5},{5,7},{10,8},{8,10},{11,... | collective-permute-start | bytes 884744 | tf_op jit(solution)/shard_map/ppermute | solution.py:27
  36.1 9.6 %collective-permute-start.8 = (bf16[2,2,256,128]{3,2,1,0:T(8,128)(2,1)}, bf16[2,2,256,128]{3,2,1,0:T(8,128)(2,1)}, u32[]{:S(2)}, u32[]{:S(2)}) collective-permute-start(bf16[2,2,256,128]{3,2,1,0:T(8,128)(2,1)} %shard_map.70), channel_id=1, source_target_pairs={{4,0},{8,4},{12,8},{16,12},{20,16},{24,20},{28,24},{5,1},{9,5},{13... | collective-permute-start | bytes 786440 | tf_op jit(solution)/shard_map/ppermute | solution.py:290
  39.0 12.4 %collective-permute-start.10 = (bf16[2,2,256,128]{3,2,1,0:T(8,128)(2,1)}, bf16[2,2,256,128]{3,2,1,0:T(8,128)(2,1)}, u32[]{:S(2)}, u32[]{:S(2)}) collective-permute-start(bf16[2,2,256,128]{3,2,1,0:T(8,128)(2,1)} %get-tuple-element.54.second), channel_id=1, source_target_pairs={{4,0},{8,4},{12,8},{16,12},{20,16},{24,20},{28,24},{5,1},{9,5},{13... | collective-permute-start | bytes 786440 | tf_op jit(solution)/shard_map/ppermute | solution.py:282
  43.0 11.7 %collective-permute-start.14 = (bf16[9,64,256]{2,1,0:T(8,128)(2,1)}, bf16[9,64,256]{2,1,0:T(8,128)(2,1)S(1)}, u32[]{:S(2)}, u32[]{:S(2)}) collective-permute-start(bf16[9,64,256]{2,1,0:T(8,128)(2,1)} %get-tuple-element.119.refs_0_), channel_id=1, source_target_pairs={{1,0},{0,1},{3,2},{2,3},{5,4},{4,5},{7,6},{6,7},{9,8},{8,9},{11,10... | collective-permute-start | bytes 884744 | tf_op jit(solution)/shard_map/ppermute | solution.py:27
  44.9 9.9 %collective-permute-start.19 = (bf16[9,64,256]{2,1,0:T(8,128)(2,1)S(1)}, bf16[9,64,256]{2,1,0:T(8,128)(2,1)S(1)}, u32[]{:S(2)}, u32[]{:S(2)}) collective-permute-start(bf16[9,64,256]{2,1,0:T(8,128)(2,1)S(1)} %get-tuple-element.118.refs_0_), channel_id=1, source_target_pairs={{1,0},{0,1},{3,2},{2,3},{5,4},{4,5},{7,6},{6,7},{9,8},{8,9},{11,10... | collective-permute-start | bytes 884744 | tf_op jit(solution)/shard_map/ppermute | solution.py:27
  45.0 10.3 %collective-permute-start.16 = (bf16[9,64,256]{2,1,0:T(8,128)(2,1)}, bf16[9,64,256]{2,1,0:T(8,128)(2,1)S(1)}, u32[]{:S(2)}, u32[]{:S(2)}) collective-permute-start(bf16[9,64,256]{2,1,0:T(8,128)(2,1)} %collective-permute-done.15.refs_2_), channel_id=1, source_target_pairs={{1,0},{0,1},{3,2},{2,3},{5,4},{4,5},{7,6},{6,7},{9,8},{8,9},{11,10... | collective-permute-start | bytes 884744 | tf_op jit(solution)/shard_map/ppermute | solution.py:27
  45.8 9.6 %collective-permute-start.17 = (bf16[2,2,256,128]{3,2,1,0:T(8,128)(2,1)}, bf16[2,2,256,128]{3,2,1,0:T(8,128)(2,1)S(1)}, u32[]{:S(2)}, u32[]{:S(2)}) collective-permute-start(bf16[2,2,256,128]{3,2,1,0:T(8,128)(2,1)} %get-tuple-element.54.second), channel_id=1, source_target_pairs={{2,0},{0,2},{3,1},{1,3},{6,4},{4,6},{7,5},{5,7},{10,8},{8,10},{11,... | collective-permute-start | bytes 786440 | tf_op jit(solution)/shard_map/ppermute | solution.py:27
  55.3 9.7 %collective-permute-start.18 = (bf16[2,2,256,128]{3,2,1,0:T(8,128)(2,1)S(1)}, bf16[2,2,256,128]{3,2,1,0:T(8,128)(2,1)S(1)}, u32[]{:S(2)}, u32[]{:S(2)}) collective-permute-start(bf16[2,2,256,128]{3,2,1,0:T(8,128)(2,1)S(1)} %collective-permute-done.17.refs_0_), channel_id=1, source_target_pairs={{1,0},{0,1},{3,2},{2,3},{5,4},{4,5},{7,6},{6,7},{9,8},{8,9},{11,10... | collective-permute-start | bytes 786440 | tf_op jit(solution)/shard_map/ppermute | solution.py:27
  62.1 13.8 %collective-permute-start.26 = (bf16[2,2,256,128]{3,2,1,0:T(8,128)(2,1)S(1)}, bf16[2,2,256,128]{3,2,1,0:T(8,128)(2,1)S(1)}, u32[]{:S(2)}, u32[]{:S(2)}) collective-permute-start(bf16[2,2,256,128]{3,2,1,0:T(8,128)(2,1)S(1)} %maximum_select_fusion.2.refs_0_.first), channel_id=1, source_target_pairs={{2,0},{0,2},{3,1},{1,3},{6,4},{4,6},{7,5},{5,7},{10,8},{8,10},{11,... | collective-permute-start | bytes 786440 | tf_op jit(solution)/shard_map/ppermute | solution.py:27
  69.1 10.4 %collective-permute-start.22 = (bf16[2,2,256,128]{3,2,1,0:T(8,128)(2,1)S(1)}, bf16[2,2,256,128]{3,2,1,0:T(8,128)(2,1)S(1)}, u32[]{:S(2)}, u32[]{:S(2)}) collective-permute-start(bf16[2,2,256,128]{3,2,1,0:T(8,128)(2,1)S(1)} %shard_map.76), channel_id=1, source_target_pairs={{4,0},{8,4},{12,8},{16,12},{20,16},{24,20},{28,24},{5,1},{9,5},{13... | collective-permute-start | bytes 786440 | tf_op jit(solution)/shard_map/ppermute | solution.py:290
  71.1 14.0 %collective-permute-start.24 = (bf16[2,2,256,128]{3,2,1,0:T(8,128)(2,1)S(1)}, bf16[2,2,256,128]{3,2,1,0:T(8,128)(2,1)S(1)}, u32[]{:S(2)}, u32[]{:S(2)}) collective-permute-start(bf16[2,2,256,128]{3,2,1,0:T(8,128)(2,1)S(1)} %get-tuple-element.61.second), channel_id=1, source_target_pairs={{4,0},{8,4},{12,8},{16,12},{20,16},{24,20},{28,24},{5,1},{9,5},{13... | collective-permute-start | bytes 786440 | tf_op jit(solution)/shard_map/ppermute | solution.py:282
  74.6 11.7 %collective-permute-start.28 = (bf16[2,2,256,128]{3,2,1,0:T(8,128)(2,1)S(1)}, bf16[2,2,256,128]{3,2,1,0:T(8,128)(2,1)S(1)}, u32[]{:S(2)}, u32[]{:S(2)}) collective-permute-start(bf16[2,2,256,128]{3,2,1,0:T(8,128)(2,1)S(1)} %get-tuple-element.61.second), channel_id=1, source_target_pairs={{2,0},{0,2},{3,1},{1,3},{6,4},{4,6},{7,5},{5,7},{10,8},{8,10},{11,... | collective-permute-start | bytes 786440 | tf_op jit(solution)/shard_map/ppermute | solution.py:27
  75.9 11.7 %collective-permute-start.27 = (bf16[2,2,256,128]{3,2,1,0:T(8,128)(2,1)S(1)}, bf16[2,2,256,128]{3,2,1,0:T(8,128)(2,1)S(1)}, u32[]{:S(2)}, u32[]{:S(2)}) collective-permute-start(bf16[2,2,256,128]{3,2,1,0:T(8,128)(2,1)S(1)} %collective-permute-done.26.refs_0_), channel_id=1, source_target_pairs={{1,0},{0,1},{3,2},{2,3},{5,4},{4,5},{7,6},{6,7},{9,8},{8,9},{11,10... | collective-permute-start | bytes 786440 | tf_op jit(solution)/shard_map/ppermute | solution.py:27
  79.5 10.7 %collective-permute-start.23 = (bf16[2,2,256,128]{3,2,1,0:T(8,128)(2,1)S(1)}, bf16[2,2,256,128]{3,2,1,0:T(8,128)(2,1)S(1)}, u32[]{:S(2)}, u32[]{:S(2)}) collective-permute-start(bf16[2,2,256,128]{3,2,1,0:T(8,128)(2,1)S(1)} %maximum_select_fusion.1.refs_0_.first), channel_id=1, source_target_pairs={{1,0},{0,1},{3,2},{2,3},{5,4},{4,5},{7,6},{6,7},{9,8},{8,9},{11,10... | collective-permute-start | bytes 786440 | tf_op jit(solution)/shard_map/ppermute | solution.py:27
  86.4 16.3 %collective-permute-start.34 = (bf16[2,2,256,128]{3,2,1,0:T(8,128)(2,1)S(1)}, bf16[2,2,256,128]{3,2,1,0:T(8,128)(2,1)S(1)}, u32[]{:S(2)}, u32[]{:S(2)}) collective-permute-start(bf16[2,2,256,128]{3,2,1,0:T(8,128)(2,1)S(1)} %maximum_select_fusion.1.refs_0_.first), channel_id=1, source_target_pairs={{2,0},{0,2},{3,1},{1,3},{6,4},{4,6},{7,5},{5,7},{10,8},{8,10},{11,... | collective-permute-start | bytes 786440 | tf_op jit(solution)/shard_map/ppermute | solution.py:27
  96.8 10.0 %collective-permute-start.30 = (bf16[2,2,256,128]{3,2,1,0:T(8,128)(2,1)S(1)}, bf16[2,2,256,128]{3,2,1,0:T(8,128)(2,1)S(1)}, u32[]{:S(2)}, u32[]{:S(2)}) collective-permute-start(bf16[2,2,256,128]{3,2,1,0:T(8,128)(2,1)S(1)} %shard_map.80), channel_id=1, source_target_pairs={{4,0},{8,4},{12,8},{16,12},{20,16},{24,20},{28,24},{5,1},{9,5},{13... | collective-permute-start | bytes 786440 | tf_op jit(solution)/shard_map/ppermute | solution.py:290
  98.8 13.6 %collective-permute-start.32 = (bf16[2,2,256,128]{3,2,1,0:T(8,128)(2,1)S(1)}, bf16[2,2,256,128]{3,2,1,0:T(8,128)(2,1)S(1)}, u32[]{:S(2)}, u32[]{:S(2)}) collective-permute-start(bf16[2,2,256,128]{3,2,1,0:T(8,128)(2,1)S(1)} %get-tuple-element.71.second), channel_id=1, source_target_pairs={{4,0},{8,4},{12,8},{16,12},{20,16},{24,20},{28,24},{5,1},{9,5},{13... | collective-permute-start | bytes 786440 | tf_op jit(solution)/shard_map/ppermute | solution.py:282
  102.4 11.9 %collective-permute-start.36 = (bf16[2,2,256,128]{3,2,1,0:T(8,128)(2,1)S(1)}, bf16[2,2,256,128]{3,2,1,0:T(8,128)(2,1)S(1)}, u32[]{:S(2)}, u32[]{:S(2)}) collective-permute-start(bf16[2,2,256,128]{3,2,1,0:T(8,128)(2,1)S(1)} %get-tuple-element.71.second), channel_id=1, source_target_pairs={{2,0},{0,2},{3,1},{1,3},{6,4},{4,6},{7,5},{5,7},{10,8},{8,10},{11,... | collective-permute-start | bytes 786440 | tf_op jit(solution)/shard_map/ppermute | solution.py:27
  102.7 12.0 %collective-permute-start.35 = (bf16[2,2,256,128]{3,2,1,0:T(8,128)(2,1)S(1)}, bf16[2,2,256,128]{3,2,1,0:T(8,128)(2,1)S(1)}, u32[]{:S(2)}, u32[]{:S(2)}) collective-permute-start(bf16[2,2,256,128]{3,2,1,0:T(8,128)(2,1)S(1)} %collective-permute-done.34.refs_0_), channel_id=1, source_target_pairs={{1,0},{0,1},{3,2},{2,3},{5,4},{4,5},{7,6},{6,7},{9,8},{8,9},{11,10... | collective-permute-start | bytes 786440 | tf_op jit(solution)/shard_map/ppermute | solution.py:27
  106.8 11.4 %collective-permute-start.31 = (bf16[2,2,256,128]{3,2,1,0:T(8,128)(2,1)S(1)}, bf16[2,2,256,128]{3,2,1,0:T(8,128)(2,1)S(1)}, u32[]{:S(2)}, u32[]{:S(2)}) collective-permute-start(bf16[2,2,256,128]{3,2,1,0:T(8,128)(2,1)S(1)} %maximum_select_fusion.refs_0_.first), channel_id=1, source_target_pairs={{1,0},{0,1},{3,2},{2,3},{5,4},{4,5},{7,6},{6,7},{9,8},{8,9},{11,10... | collective-permute-start | bytes 786440 | tf_op jit(solution)/shard_map/ppermute | solution.py:27
  114.0 8.0 %collective-permute-start.40 = (bf16[2,2,256,128]{3,2,1,0:T(8,128)(2,1)S(1)}, bf16[2,2,256,128]{3,2,1,0:T(8,128)(2,1)S(1)}, u32[]{:S(2)}, u32[]{:S(2)}) collective-permute-start(bf16[2,2,256,128]{3,2,1,0:T(8,128)(2,1)S(1)} %maximum_select_fusion.refs_0_.first), channel_id=1, source_target_pairs={{2,0},{0,2},{3,1},{1,3},{6,4},{4,6},{7,5},{5,7},{10,8},{8,10},{11,... | collective-permute-start | bytes 786440 | tf_op jit(solution)/shard_map/ppermute | solution.py:27
  114.3 8.5 %collective-permute-start.37 = (bf16[2,2,256,128]{3,2,1,0:T(8,128)(2,1)S(1)}, bf16[2,2,256,128]{3,2,1,0:T(8,128)(2,1)S(1)}, u32[]{:S(2)}, u32[]{:S(2)}) collective-permute-start(bf16[2,2,256,128]{3,2,1,0:T(8,128)(2,1)S(1)} %collective-permute-done.36.refs_0_), channel_id=1, source_target_pairs={{1,0},{0,1},{3,2},{2,3},{5,4},{4,5},{7,6},{6,7},{9,8},{8,9},{11,10... | collective-permute-start | bytes 786440 | tf_op jit(solution)/shard_map/ppermute | solution.py:27
  122.0 9.0 %collective-permute-start.41 = (bf16[2,2,256,128]{3,2,1,0:T(8,128)(2,1)S(1)}, bf16[2,2,256,128]{3,2,1,0:T(8,128)(2,1)S(1)}, u32[]{:S(2)}, u32[]{:S(2)}) collective-permute-start(bf16[2,2,256,128]{3,2,1,0:T(8,128)(2,1)S(1)} %collective-permute-done.40.refs_0_), channel_id=1, source_target_pairs={{1,0},{0,1},{3,2},{2,3},{5,4},{4,5},{7,6},{6,7},{9,8},{8,9},{11,10... | collective-permute-start | bytes 786440 | tf_op jit(solution)/shard_map/ppermute | solution.py:27
  (30 other events, 149.7 us)
where the time goes:
time: 138 us
  starting transfers between devices  47.7 us (35%)
  Pallas kernels  44.8 us (32%)
  waiting for transfers between devices  25.3 us (18%)
  local copies, waits for them, and re-layouts  11.6 us (8%)
  other arithmetic  6.97 us (5%)
    pallas_call x20, Pallas kernels, call(): pl.pallas_call(body, out_shape=outs, in_specs=[SMEM] + [VMEM] * (len(inpu...  44.8 us
    ppermute x36, starting transfers between devices, around(): lax.ppermute(shard, axis, ring(axis, k))  31.6 us
    ppermute x3, waiting for transfers between devices, local(): lax.ppermute(middle, 'section', down)  10.8 us
    ppermute x3, starting transfers between devices, local(): lax.ppermute(middle, 'section', down)  10.2 us
    ppermute x36, waiting for transfers between devices, around(): lax.ppermute(shard, axis, ring(axis, k))  9.07 us
    ppermute x3, starting transfers between devices, local(): lax.ppermute(last, 'section', down)  5.97 us
    ppermute x3, waiting for transfers between devices, local(): lax.ppermute(last, 'section', down)  5.41 us
    unnamed x41, local copies, waits for them, and re-layouts  5.05 us
  transfers between devices with their start and end apart: 42, of which 9 were waited for; matrix products, arithmetic and copies ran while one was open for 8% of the time, Pallas kernels for 31%

commit v1 on v0

--- a/solution.py
+++ b/solution.py
@@ -6,7 +6,9 @@
 from jax import lax
 from jax.experimental import pallas as pl
 from jax.experimental.pallas import tpu as pltpu
+from jax.experimental.layout import Layout, with_layout_constraint
 from jax.sharding import PartitionSpec as P
+
 
 learn_rate = 0.05
 momentum_decay = 0.9
@@ -111,26 +113,31 @@
     count = pieces * (images - 1)
     given, refs = refs[:count], refs[count:]
     if final:
-        params, moments, params_out, moments_out, act, cot, moved = refs
+        params, moments = refs[:2]
+        params_out, moments_out, act, cot, moved = refs[-5:]
+        params_out, moments_out = params_out.at[0], moments_out.at[0]
     else:
         (weights, speed, params, moments, weights_out, flip_out, speed_out, params_out,
          moments_out, act, cot, moved, total) = refs
     me, mine = place[0], place[1]
+    if len(params.shape) == 4:
+        params, moments = params.at[0], moments.at[0]
     rows = padded.shape[1] - 2
     band = rows // pieces
     channels = padded.shape[2]
     part = params.shape[1]
+    slot = pl.ds(pl.multiple_of(mine * part, part), part)
+    kept = slot if final else slice(None)
     for r in range(rows):
         act[r] = padded[0, r + 1]
-        cot[r] = padded[1, r + 1]
+        cot[r] = padded[1, r + 1, kept, :]
     for image in range(images - 1):
         for s in range(pieces):
             piece = given[image * pieces + s]
             start = (image + 1) * rows + lax.rem(me + s, pieces) * band
             for r in range(band):
                 act[start + r] = silu16(piece[0, r])
-                cot[start + r] = piece[1, r]
-    slot = pl.ds(pl.multiple_of(mine * part, part), part)
+                cot[start + r] = piece[1, r, kept, :]
     for b in range(3):
         source = cot
         if b != 1:
@@ -144,10 +151,7 @@
                 for r in range(rows)
                 if 0 <= r + a - 1 < rows
             ]
-            if final:
-                left = jnp.concatenate([source[r, slot, :] for r, _ in valid], axis=1)
-            else:
-                left = jnp.concatenate([source[r] for r, _ in valid], axis=1)
+            left = jnp.concatenate([source[r] for r, _ in valid], axis=1)
             right = jnp.concatenate([act[r] for _, r in valid], axis=1)
             grad = lax.dot_general(
                 left, right, (((1,), (1,)), ((), ())), preferred_element_type=f32
@@ -192,16 +196,33 @@
                 flip[2 - b, :, (2 - a) * channels : (3 - a) * channels] = block.T.astype(bf16)
 
 
-def call(body, outs, inputs, flops, scratch=()):
+def call(body, outs, inputs, flops, scratch=(), slot=None, aliases=0, read=None):
     size = sum(math.prod(x.shape) * x.dtype.itemsize for x in list(inputs) + list(outs))
+    extra, in_out = {}, {}
+    out_specs = [VMEM] * len(outs)
+
+    def half(x, which):
+        return pl.BlockSpec((1,) + x.shape[1:], lambda i, n=len(x.shape): (which,) + (0,) * (n - 1))
+
+    if slot is not None or read is not None:
+        extra["grid"] = (1,)
+    if slot is not None:
+        out_specs = [half(x, slot) for x in outs]
+        in_out = {len(inputs) - aliases + k: k for k in range(aliases)}
+    in_specs = [SMEM] + [VMEM] * (len(inputs) - 1 - aliases)
+    if read is not None:
+        in_specs[-2:] = [half(x, read) for x in inputs[-2:]]
+    in_specs += [pl.BlockSpec(memory_space=pl.ANY)] * aliases
     return pl.pallas_call(
         body,
         out_shape=outs,
-        in_specs=[SMEM] + [VMEM] * (len(inputs) - 1),
-        out_specs=[VMEM] * len(outs),
+        in_specs=in_specs,
+        out_specs=out_specs,
         scratch_shapes=list(scratch),
+        input_output_aliases=in_out,
         compiler_params=pltpu.CompilerParams(vmem_limit_bytes=32 * 1024 * 1024),
         cost_estimate=pl.CostEstimate(flops=flops, bytes_accessed=size, transcendentals=0),
+        **extra,
     )(*inputs)
 
 
@@ -216,23 +237,27 @@
     top_section = lax.axis_index("section") == sections - 1
     me, at = lax.axis_index("spatial"), lax.axis_index("dp")
     place = jnp.stack([me, at * pieces + me, at]).astype(jnp.int32)
-    shape = functools.partial(jax.ShapeDtypeStruct)
+    shape = jax.ShapeDtypeStruct
     message = shape((2, band, channels, width), bf16)
     padded = shape((2, rows + 2, channels, width), bf16)
     block = shape((3, channels, 3 * channels), bf16)
     conv_flops = 2 * 2 * 9 * channels * channels * rows * width
-    share = params.shape[3]
 
     def rowwise(stack, members):
         return jnp.stack([jnp.swapaxes(stack[m, 0], 0, 1) for m in members])
 
-    def gathered(shard, flipping):
-        parts = [q for p in around(shard, "dp") for q in around(p, "spatial")]
+    def abroad(shard):
+        return around(shard, "dp")[1:]
+
+    def spread(parts):
+        return [q for p in parts for q in around(p, "spatial")]
+
+    def assembled(parts, flipping):
         body = functools.partial(assemble, images, pieces, flipping)
         return call(body, [block] * (2 if flipping else 1), [place] + parts, channels**3)
 
     def one(first, second, kernel, flip):
-        inputs = [place] + around(first, "spatial") + second + [kernel, flip]
+        inputs = [place] + first + second + [kernel, flip]
         scratch = [pltpu.VMEM((rows, channels, width), bf16), pltpu.VMEM((2, rows, channels, width), bf16)]
         return call(
             functools.partial(stage_one, pieces), [padded, padded, message], inputs, conv_flops, scratch
@@ -242,68 +267,104 @@
         inputs = [place, padded_b, first, second, kernel, flip]
         return call(stage_two, [message], inputs, conv_flops // pieces)[0]
 
-    def abroad(shard):
-        return [q for p in around(shard, "dp")[1:] for q in around(p, "spatial")]
-
-    def learn(padded_own, others, state, final):
+    def learn(padded_own, others, state, slot=None, pair=(), read=None):
         weights, speed, own_params, own_moments = state
-        own = shape(own_params.shape, f32)
-        field = pltpu.VMEM((images * rows, channels, width), bf16)
-        scratch = [field] * 3
-        outs = [own, own]
+        final = slot is not None
+        share = own_params.shape[-2]
+        depths = (channels, share, share) if final else (channels,) * 3
+        scratch = [pltpu.VMEM((images * rows, depth, width), bf16) for depth in depths]
         inputs = [place, padded_own] + others
         if final:
-            inputs += [own_params, own_moments]
+            outs = [shape((2,) + own_params.shape, f32)] * 2
+            inputs += [own_params, own_moments, *pair]
         else:
             inputs += [weights, speed, own_params, own_moments]
-            outs = [block] * 3 + outs
+            outs = [block] * 3 + [shape(own_params.shape[-3:], f32)] * 2
             scratch += [pltpu.VMEM((channels, channels), f32)]
         body = functools.partial(update, pieces, images, final, scale)
         flops = 2 * 9 * channels * channels * rows * width * images
-        return call(body, outs, inputs, flops, scratch)
-
+        return call(body, outs, inputs, flops, scratch, slot, len(pair), read)
+
+    kernel_g = (params[0, 1] * scale).astype(bf16)
+    far_g = abroad(kernel_g)
+    own_g = around(kernel_g, "spatial")
+    kernel_f = (params[0, 0] * scale).astype(bf16)
+    far_f = abroad(kernel_f)
+    own_f = around(kernel_f, "spatial")
     first = rowwise(inbox[0], (0, 3))
     second = rowwise(inbox[0], (1, 2))
-    kernels = (params[0] * scale).astype(bf16)
+    first, second = lax.optimization_barrier((first, second))
+    first_all = around(first, "spatial")
+    second_all = around(second, "spatial")
+    far_a = abroad(first)
     speeds = moments[0].astype(bf16)
-    weights_g, flip_g = gathered(kernels[1], True)
-    weights_f, flip_f = gathered(kernels[0], True)
-    (speed_g,) = gathered(speeds[1], False)
-    (speed_f,) = gathered(speeds[0], False)
-    params_f, params_g = params[0, 0], params[0, 1]
-    moments_f, moments_g = moments[0, 0], moments[0, 1]
+    far_mg = abroad(speeds[1])
+    far_mf = abroad(speeds[0])
+    own_mg, own_mf = around(speeds[1], "spatial"), around(speeds[0], "spatial")
+    far_g = spread(far_g)
+    weights_g, flip_g = assembled(own_g + far_g, True)
+    far_f = spread(far_f)
+    weights_f, flip_f = assembled(own_f + far_f, True)
+    params_f = params_g = params[0]
+    moments_f = moments_g = moments[0]
     down = [(i, i - 1) for i in range(1, sections)]
-    second_all = around(second, "spatial")
     for tick in range(ticks):
         final = tick == ticks - 1
-        padded_a, padded_b, middle = one(first, second_all, weights_g, flip_g)
+        padded_a, padded_b, middle = one(first_all, second_all, weights_g, flip_g)
         if not final:
-            second = jnp.where(
-                top_section, rowwise(fresh[tick], (1, 2)), lax.ppermute(middle, "section", down)
+            second = lax.ppermute(middle, "section", down)
+        far_b = abroad(middle)
+        if tick == 1:
+            held, _ = lax.optimization_barrier((held, middle))
+            weights_f, flip_f, speed_f, params_f, moments_f = learn(
+                held, others_f, (weights_f, speed_f, params_f, moments_f), read=0
             )
+        last = two(padded_b, first, middle, weights_f, flip_f)
+        if not final:
+            following = lax.ppermute(last, "section", down)
+            given, _ = lax.optimization_barrier((fresh, last))
+            later = lax.optimization_barrier(
+                (rowwise(given[tick], (0, 3)), rowwise(given[tick], (1, 2)))
+            )
+        else:
+            sent = jnp.stack([last[0], middle[0], middle[1], last[1]])
+            outbox = jnp.swapaxes(sent, 1, 2)[None, :, None]
+            outbox = with_layout_constraint(outbox, Layout(tuple(range(outbox.ndim))))
+            outbox, far_a = lax.optimization_barrier((outbox, far_a))
+        others_g = spread(far_a)
+        if tick == 0:
+            far_mg = spread(far_mg)
+            (speed_g,) = assembled(own_mg + far_mg, False)
+        state_g = (None, None, params_g, moments_g) if final else (
+            weights_g, speed_g, params_g, moments_g
+        )
+        if final:
+            pair = learn(padded_a, others_g, state_g, 1)
+        else:
+            weights_g, flip_g, speed_g, params_g, moments_g = learn(
+                padded_a, others_g, state_g, read=1 if tick == 0 else None
+            )
+        if not final:
+            second = jnp.where(top_section, later[1], second)
             second_all = around(second, "spatial")
-        last = two(padded_b, first, middle, weights_f, flip_f)
-        others_g = abroad(first)
-        others_f = abroad(middle)
+        others_f = spread(far_b)
         if not final:
-            first = jnp.where(
-                top_section, rowwise(fresh[tick], (0, 3)), lax.ppermute(last, "section", down)
-            )
-        state_g = (weights_g, speed_g, params_g, moments_g)
-        state_f = (weights_f, speed_f, params_f, moments_f)
+            first = jnp.where(top_section, later[0], following)
+            first_all = around(first, "spatial")
+            far_a = abroad(first)
+        if tick == 0:
+            far_mf = spread(far_mf)
+            (speed_f,) = assembled(own_mf + far_mf, False)
+        if tick == 0:
+            held = padded_b
+            continue
         if final:
-            params_g, moments_g = learn(padded_a, others_g, state_g, True)
-            params_f, moments_f = learn(padded_b, others_f, state_f, True)
+            state_f = (None, None, params_f, moments_f)
+            params_out, moments_out = learn(padded_b, others_f, state_f, 0, pair)
         else:
-            weights_g, flip_g, speed_g, params_g, moments_g = learn(padded_a, others_g, state_g, False)
-            weights_f, flip_f, speed_f, params_f, moments_f = learn(padded_b, others_f, state_f, False)
-    sent = jnp.stack([last[0], middle[0], middle[1], last[1]])
-    outbox = jnp.swapaxes(sent, 1, 2)[None, :, None]
-    return (
-        outbox,
-        jnp.stack([params_f, params_g])[None],
-        jnp.stack([moments_f, moments_g])[None],
-    )
+            state_f = (weights_f, speed_f, params_f, moments_f)
+            weights_f, flip_f, speed_f, params_f, moments_f = learn(padded_b, others_f, state_f)
+    return outbox, params_out[None], moments_out[None]
 
 
 def solution(mesh):

time: 138 us -> 132 us (0.957)
  local copies, waits for them, and re-layouts: 11.6 us -> 4 us
  waiting for transfers between devices: 25.3 us -> 31.1 us
  other arithmetic: 6.97 us -> 5.09 us
    unnamed x41 -> x10, local copies, waits for them, and re-layouts: 5.05 us -> 1.11 us
    slice x2 -> x1, local copies, waits for them, and re-layouts: 3.82 us -> 0.36 us  [rowwise(): return jnp.stack([jnp.swapaxes(stack[m, 0], 0, 1) for m in members])]
    ppermute x36, waiting for transfers between devices: 9.07 us -> 12.1 us  [around(): lax.ppermute(shard, axis, ring(axis, k))]
    ppermute x6, waiting for transfers between devices: 16.2 us -> 19 us  [the longest x3 10.7 us: local(): second = lax.ppermute(middle, 'section', down)]
    broadcast_in_dim x2 -> x0, other arithmetic: 2.23 us -> none  [the longest x1 1.12 us: local(): jnp.stack([params_f, params_g])[None]]
    select_n x6, other arithmetic: 2.31 us -> 0.17 us  [the longest x3 0.09 us: local(): second = jnp.where(top_section, later[1], second)]
    another operation x8 -> x5, local copies, waits for them, and re-layouts: 1.71 us -> 0.18 us  [rowwise(): return jnp.stack([jnp.swapaxes(stack[m, 0], 0, 1) for m in members])]
    broadcast_in_dim x1, other arithmetic: 0.06 us -> 1.59 us  [local(): outbox = jnp.swapaxes(sent, 1, 2)[None, :, None]]
  transfers between devices with their start and end apart: 42 -> 42, of which waited for: 9 -> 9; matrix products, arithmetic and copies ran while one was open for 8% -> 5% of each run, Pallas kernels for 31% -> 31%
where the time goes in v1:
time: 132 us; the launch traced here: 131 us
  starting transfers between devices  46.5 us (35%)
  Pallas kernels  43.5 us (33%)
  waiting for transfers between devices  31.1 us (24%)
  other arithmetic  5.09 us (4%)
  local copies, waits for them, and re-layouts  4 us (3%)
    pallas_call x20, Pallas kernels, call(): pl.pallas_call(body, out_shape=outs, in_specs=in_specs, out_specs=out_spe...  43.5 us
    ppermute x36, starting transfers between devices, around(): lax.ppermute(shard, axis, ring(axis, k))  30.7 us
    ppermute x36, waiting for transfers between devices, around(): lax.ppermute(shard, axis, ring(axis, k))  12.1 us
    ppermute x3, waiting for transfers between devices, local(): second = lax.ppermute(middle, 'section', down)  10.7 us
    ppermute x3, waiting for transfers between devices, local(): following = lax.ppermute(last, 'section', down)  8.3 us
    ppermute x3, starting transfers between devices, local(): second = lax.ppermute(middle, 'section', down)  8.14 us
    ppermute x3, starting transfers between devices, local(): following = lax.ppermute(last, 'section', down)  7.75 us
  transfers between devices with their start and end apart: 42, of which 9 were waited for; matrix products, arithmetic and copies ran while one was open for 5% of the time, Pallas kernels for 31%

profile of v1, /device:TPU:21, one launch (start us, length us, event | category | flops | bytes accessed | tf_op | source)
XLA Modules:
  0.0 131.4 jit_solution(7105542280239599829)
XLA Ops:
  7.5 2.6 %collective-permute-done.6.refs_2_ = bf16[9,64,256]{2,1,0:T(8,128)(2,1)S(1)} collective-permute-done((bf16[9,64,256]{2,1,0:T(8,128)(2,1)S(1)}, bf16[9,64,256]{2,1,0:T(8,128)(2,1)S(1)}, u32[]{:S(2)}, u32[]{:S(2)}) %collective-permute-start.6) | collective-permute-done | bytes 294944 | tf_op jit(solution)/shard_map/ppermute | solution.py:29
  10.0 2.7 %collective-permute-start = (bf16[2,2,256,128]{3,2,1,0:T(8,128)(2,1)S(1)}, bf16[2,2,256,128]{3,2,1,0:T(8,128)(2,1)}, u32[]{:S(2)}, u32[]{:S(2)}) collective-permute-start(bf16[2,2,256,128]{3,2,1,0:T(8,128)(2,1)S(1)} %pad_maximum_fusion.refs_0_.first), channel_id=1, source_target_pairs={{1,0},{0,1},{3,2},{2,3},{5,4},{4,5},{7,6},{6,7},{9,8},{8,9},{11,10... | collective-permute-start | bytes 786440 | tf_op jit(solution)/shard_map/ppermute | solution.py:29
  12.7 3.7 %collective-permute-done.3.refs_2_ = bf16[9,64,256]{2,1,0:T(8,128)(2,1)S(1)} collective-permute-done((bf16[9,64,256]{2,1,0:T(8,128)(2,1)S(1)}, bf16[9,64,256]{2,1,0:T(8,128)(2,1)S(1)}, u32[]{:S(2)}, u32[]{:S(2)}) %collective-permute-start.3) | collective-permute-done | bytes 294944 | tf_op jit(solution)/shard_map/ppermute | solution.py:29
  16.4 1.5 %collective-permute-start.7 = (bf16[9,64,256]{2,1,0:T(8,128)(2,1)S(1)}, bf16[9,64,256]{2,1,0:T(8,128)(2,1)S(1)}, u32[]{:S(2)}, u32[]{:S(2)}) collective-permute-start(bf16[9,64,256]{2,1,0:T(8,128)(2,1)S(1)} %collective-permute-done.6.refs_2_), channel_id=1, source_target_pairs={{1,0},{0,1},{3,2},{2,3},{5,4},{4,5},{7,6},{6,7},{9,8},{8,9},{11,10... | collective-permute-start | bytes 884744 | tf_op jit(solution)/shard_map/ppermute | solution.py:29
  20.9 1.5 %shard_map.67 = (bf16[3,256,768]{2,1,0:T(8,128)(2,1)S(1)}, bf16[3,256,768]{2,1,0:T(8,128)(2,1)S(1)}) custom-call(s32[3]{0:T(128)S(1)} %pad_add_fusion.place, bf16[9,64,256]{2,1,0:T(8,128)(2,1)S(1)} %get-tuple-element.140.refs_0_, bf16[9,64,256]{2,1,0:T(8,128)(2,1)S(1)} %collective-permute-done.2.refs_1_, ...), custom_call_target="tpu_custom_call" | custom-call | flops 16777216 | bytes 3538956 | tf_op jit(solution)/shard_map/pallas_call | solution.py:216
  26.0 3.1 %shard_map.68 = (bf16[2,6,256,128]{3,2,1,0:T(8,128)(2,1)S(1)}, bf16[2,6,256,128]{3,2,1,0:T(8,128)(2,1)S(1)}, bf16[2,2,256,128]{3,2,1,0:T(8,128)(2,1)S(1)}) custom-call(s32[3]{0:T(128)S(1)} %pad_add_fusion.place, bf16[2,2,256,128]{3,2,1,0:T(8,128)(2,1)S(1)} %pad_maximum_fusion.refs_0_.first, bf16[2,2,256,128]{3,2,1,0:T(8,128)(2,1)} %collective-permute-done.refs_1_, ...), custom_call_target="tpu_custom_call" | custom-call | flops 1207959552 | bytes 5242892 | tf_op jit(solution)/shard_map/pallas_call | solution.py:216
  30.5 2.2 %collective-permute-start.8 = (bf16[2,2,256,128]{3,2,1,0:T(8,128)(2,1)S(1)}, bf16[2,2,256,128]{3,2,1,0:T(8,128)(2,1)S(1)}, u32[]{:S(2)}, u32[]{:S(2)}) collective-permute-start(bf16[2,2,256,128]{3,2,1,0:T(8,128)(2,1)S(1)} %shard_map.70), channel_id=1, source_target_pairs={{4,0},{8,4},{12,8},{16,12},{20,16},{24,20},{28,24},{5,1},{9,5},{13... | collective-permute-start | bytes 786440 | tf_op jit(solution)/shard_map/ppermute | solution.py:324
  33.1 3.0 %collective-permute-start.10 = (bf16[2,2,256,128]{3,2,1,0:T(8,128)(2,1)S(1)}, bf16[2,2,256,128]{3,2,1,0:T(8,128)(2,1)S(1)}, u32[]{:S(2)}, u32[]{:S(2)}) collective-permute-start(bf16[2,2,256,128]{3,2,1,0:T(8,128)(2,1)S(1)} %get-tuple-element.70.second), channel_id=1, source_target_pairs={{4,0},{8,4},{12,8},{16,12},{20,16},{24,20},{28,24},{5,1},{9,5},{13... | collective-permute-start | bytes 786440 | tf_op jit(solution)/shard_map/ppermute | solution.py:315
  37.1 3.8 %collective-permute-done.8 = bf16[2,2,256,128]{3,2,1,0:T(8,128)(2,1)S(1)} collective-permute-done((bf16[2,2,256,128]{3,2,1,0:T(8,128)(2,1)S(1)}, bf16[2,2,256,128]{3,2,1,0:T(8,128)(2,1)S(1)}, u32[]{:S(2)}, u32[]{:S(2)}) %collective-permute-start.8) | collective-permute-done | bytes 262176 | tf_op jit(solution)/shard_map/ppermute | solution.py:324
  40.9 1.9 %collective-permute-start.21 = (bf16[9,64,256]{2,1,0:T(8,128)(2,1)S(1)}, bf16[9,64,256]{2,1,0:T(8,128)(2,1)S(1)}, u32[]{:S(2)}, u32[]{:S(2)}) collective-permute-start(bf16[9,64,256]{2,1,0:T(8,128)(2,1)S(1)} %collective-permute-done.20.refs_2_), channel_id=1, source_target_pairs={{1,0},{0,1},{3,2},{2,3},{5,4},{4,5},{7,6},{6,7},{9,8},{8,9},{11,10... | collective-permute-start | bytes 884744 | tf_op jit(solution)/shard_map/ppermute | solution.py:29
  43.4 3.1 %collective-permute-done.10 = bf16[2,2,256,128]{3,2,1,0:T(8,128)(2,1)S(1)} collective-permute-done((bf16[2,2,256,128]{3,2,1,0:T(8,128)(2,1)S(1)}, bf16[2,2,256,128]{3,2,1,0:T(8,128)(2,1)S(1)}, u32[]{:S(2)}, u32[]{:S(2)}) %collective-permute-start.10) | collective-permute-done | bytes 262176 | tf_op jit(solution)/shard_map/ppermute | solution.py:315
  46.8 1.5 %collective-permute-start.11 = (bf16[2,2,256,128]{3,2,1,0:T(8,128)(2,1)S(1)}, bf16[2,2,256,128]{3,2,1,0:T(8,128)(2,1)S(1)}, u32[]{:S(2)}, u32[]{:S(2)}) collective-permute-start(bf16[2,2,256,128]{3,2,1,0:T(8,128)(2,1)S(1)} %broadcast_select_fusion.4.refs_2_), channel_id=1, source_target_pairs={{1,0},{0,1},{3,2},{2,3},{5,4},{4,5},{7,6},{6,7},{9,8},{8,9},{11,10... | collective-permute-start | bytes 786440 | tf_op jit(solution)/shard_map/ppermute | solution.py:29
  48.4 4.8 %collective-permute-done.17.refs_0_ = bf16[2,2,256,128]{3,2,1,0:T(8,128)(2,1)S(1)} collective-permute-done((bf16[2,2,256,128]{3,2,1,0:T(8,128)(2,1)S(1)}, bf16[2,2,256,128]{3,2,1,0:T(8,128)(2,1)S(1)}, u32[]{:S(2)}, u32[]{:S(2)}) %collective-permute-start.17) | collective-permute-done | bytes 262176 | tf_op jit(solution)/shard_map/ppermute | solution.py:29
  53.2 2.0 %collective-permute-start.18 = (bf16[2,2,256,128]{3,2,1,0:T(8,128)(2,1)S(1)}, bf16[2,2,256,128]{3,2,1,0:T(8,128)(2,1)S(1)}, u32[]{:S(2)}, u32[]{:S(2)}) collective-permute-start(bf16[2,2,256,128]{3,2,1,0:T(8,128)(2,1)S(1)} %collective-permute-done.17.refs_0_), channel_id=1, source_target_pairs={{1,0},{0,1},{3,2},{2,3},{5,4},{4,5},{7,6},{6,7},{9,8},{8,9},{11,10... | collective-permute-start | bytes 786440 | tf_op jit(solution)/shard_map/ppermute | solution.py:29
  57.1 2.5 %shard_map.72 = (bf16[3,256,768]{2,1,0:T(8,128)(2,1)S(1)}, bf16[3,256,768]{2,1,0:T(8,128)(2,1)S(1)}, bf16[3,256,768]{2,1,0:T(8,128)(2,1)S(1)}, f32[9,64,256]{2,1,0:T(8,128)S(1)}, f32[9,64,256]{2,1,0:T(8,128)S(1)}) custom-call(s32[3]{0:T(128)S(1)} %pad_add_fusion.place, bf16[2,6,256,128]{3,2,1,0:T(8,128)(2,1)S(1)} %get-tuple-element.76.padded, ...), custom_call_target="tpu_custom_call" | custom-call | flops 1207959552 | bytes 10747916 | tf_op jit(solution)/shard_map/pallas_call | solution.py:216
  60.1 2.6 %shard_map.73 = (bf16[2,6,256,128]{3,2,1,0:T(8,128)(2,1)S(1)}, bf16[2,6,256,128]{3,2,1,0:T(8,128)(2,1)S(1)}, bf16[2,2,256,128]{3,2,1,0:T(8,128)(2,1)S(1)}) custom-call(s32[3]{0:T(128)S(1)} %pad_add_fusion.place, bf16[2,2,256,128]{3,2,1,0:T(8,128)(2,1)S(1)} %broadcast_select_fusion.5.refs_0_.first, ...), custom_call_target="tpu_custom_call" | custom-call | flops 1207959552 | bytes 5242892 | tf_op jit(solution)/shard_map/pallas_call | solution.py:216
  63.9 2.1 %collective-permute-start.24 = (bf16[2,2,256,128]{3,2,1,0:T(8,128)(2,1)S(1)}, bf16[2,2,256,128]{3,2,1,0:T(8,128)(2,1)S(1)}, u32[]{:S(2)}, u32[]{:S(2)}) collective-permute-start(bf16[2,2,256,128]{3,2,1,0:T(8,128)(2,1)S(1)} %get-tuple-element.80.second), channel_id=1, source_target_pairs={{4,0},{8,4},{12,8},{16,12},{20,16},{24,20},{28,24},{5,1},{9,5},{13... | collective-permute-start | bytes 786440 | tf_op jit(solution)/shard_map/ppermute | solution.py:315
  66.0 2.6 %shard_map.75 = (bf16[3,256,768]{2,1,0:T(8,128)(2,1)S(1)}, bf16[3,256,768]{2,1,0:T(8,128)(2,1)S(1)}, bf16[3,256,768]{2,1,0:T(8,128)(2,1)S(1)}, f32[9,64,256]{2,1,0:T(8,128)S(1)}, f32[9,64,256]{2,1,0:T(8,128)S(1)}) custom-call(s32[3]{0:T(128)S(1)} %pad_add_fusion.place, bf16[2,6,256,128]{3,2,1,0:T(8,128)(2,1)S(1)} %get-tuple-element.81.padded, ...), custom_call_target="tpu_custom_call" | custom-call | flops 1207959552 | bytes 10747916 | tf_op jit(solution)/shard_map/pallas_call | solution.py:216
  70.0 3.2 %collective-permute-start.22 = (bf16[2,2,256,128]{3,2,1,0:T(8,128)(2,1)S(1)}, bf16[2,2,256,128]{3,2,1,0:T(8,128)(2,1)S(1)}, u32[]{:S(2)}, u32[]{:S(2)}) collective-permute-start(bf16[2,2,256,128]{3,2,1,0:T(8,128)(2,1)S(1)} %shard_map.76), channel_id=1, source_target_pairs={{4,0},{8,4},{12,8},{16,12},{20,16},{24,20},{28,24},{5,1},{9,5},{13... | collective-permute-start | bytes 786440 | tf_op jit(solution)/shard_map/ppermute | solution.py:324
  75.6 4.5 %collective-permute-done.22 = bf16[2,2,256,128]{3,2,1,0:T(8,128)(2,1)S(1)} collective-permute-done((bf16[2,2,256,128]{3,2,1,0:T(8,128)(2,1)S(1)}, bf16[2,2,256,128]{3,2,1,0:T(8,128)(2,1)S(1)}, u32[]{:S(2)}, u32[]{:S(2)}) %collective-permute-start.22) | collective-permute-done | bytes 262176 | tf_op jit(solution)/shard_map/ppermute | solution.py:324
  81.9 2.5 %shard_map.77 = (bf16[3,256,768]{2,1,0:T(8,128)(2,1)S(1)}, bf16[3,256,768]{2,1,0:T(8,128)(2,1)S(1)}, bf16[3,256,768]{2,1,0:T(8,128)(2,1)S(1)}, f32[9,64,256]{2,1,0:T(8,128)S(1)}, f32[9,64,256]{2,1,0:T(8,128)S(1)}) custom-call(s32[3]{0:T(128)S(1)} %pad_add_fusion.place, bf16[2,6,256,128]{3,2,1,0:T(8,128)(2,1)S(1)} %get-tuple-element.87.padded, ...), custom_call_target="tpu_custom_call" | custom-call | flops 1207959552 | bytes 9568268 | tf_op jit(solution)/shard_map/pallas_call | solution.py:216
  84.4 2.6 %shard_map.79 = (bf16[3,256,768]{2,1,0:T(8,128)(2,1)S(1)}, bf16[3,256,768]{2,1,0:T(8,128)(2,1)S(1)}, bf16[3,256,768]{2,1,0:T(8,128)(2,1)S(1)}, f32[9,64,256]{2,1,0:T(8,128)S(1)}, f32[9,64,256]{2,1,0:T(8,128)S(1)}) custom-call(s32[3]{0:T(128)S(1)} %pad_add_fusion.place, bf16[2,6,256,128]{3,2,1,0:T(8,128)(2,1)S(1)} %get-tuple-element.79.padded, ...), custom_call_target="tpu_custom_call" | custom-call | flops 1207959552 | bytes 9568268 | tf_op jit(solution)/shard_map/pallas_call | solution.py:216
  87.0 2.6 %shard_map.78 = (bf16[2,6,256,128]{3,2,1,0:T(8,128)(2,1)S(1)}, bf16[2,6,256,128]{3,2,1,0:T(8,128)(2,1)S(1)}, bf16[2,2,256,128]{3,2,1,0:T(8,128)(2,1)S(1)}) custom-call(s32[3]{0:T(128)S(1)} %pad_add_fusion.place, bf16[2,2,256,128]{3,2,1,0:T(8,128)(2,1)S(1)} %broadcast_select_fusion.3.refs_0_.first, ...), custom_call_target="tpu_custom_call" | custom-call | flops 1207959552 | bytes 5242892 | tf_op jit(solution)/shard_map/pallas_call | solution.py:216
  91.0 2.3 %collective-permute-start.30 = (bf16[2,2,256,128]{3,2,1,0:T(8,128)(2,1)S(1)}, bf16[2,2,256,128]{3,2,1,0:T(8,128)(2,1)S(1)}, u32[]{:S(2)}, u32[]{:S(2)}) collective-permute-start(bf16[2,2,256,128]{3,2,1,0:T(8,128)(2,1)S(1)} %shard_map.80), channel_id=1, source_target_pairs={{4,0},{8,4},{12,8},{16,12},{20,16},{24,20},{28,24},{5,1},{9,5},{13... | collective-permute-start | bytes 786440 | tf_op jit(solution)/shard_map/ppermute | solution.py:324
  94.6 3.0 %collective-permute-start.32 = (bf16[2,2,256,128]{3,2,1,0:T(8,128)(2,1)S(1)}, bf16[2,2,256,128]{3,2,1,0:T(8,128)(2,1)S(1)}, u32[]{:S(2)}, u32[]{:S(2)}) collective-permute-start(bf16[2,2,256,128]{3,2,1,0:T(8,128)(2,1)S(1)} %get-tuple-element.94.second), channel_id=1, source_target_pairs={{4,0},{8,4},{12,8},{16,12},{20,16},{24,20},{28,24},{5,1},{9,5},{13... | collective-permute-start | bytes 786440 | tf_op jit(solution)/shard_map/ppermute | solution.py:315
  99.4 7.6 %collective-permute-done.32 = bf16[2,2,256,128]{3,2,1,0:T(8,128)(2,1)S(1)} collective-permute-done((bf16[2,2,256,128]{3,2,1,0:T(8,128)(2,1)S(1)}, bf16[2,2,256,128]{3,2,1,0:T(8,128)(2,1)S(1)}, u32[]{:S(2)}, u32[]{:S(2)}) %collective-permute-start.32) | collective-permute-done | bytes 262176 | tf_op jit(solution)/shard_map/ppermute | solution.py:315
  110.1 3.5 %shard_map.81 = (bf16[3,256,768]{2,1,0:T(8,128)(2,1)S(1)}, bf16[3,256,768]{2,1,0:T(8,128)(2,1)S(1)}, bf16[3,256,768]{2,1,0:T(8,128)(2,1)}, f32[9,64,256]{2,1,0:T(8,128)S(1)}, f32[9,64,256]{2,1,0:T(8,128)S(1)}) custom-call(s32[3]{0:T(128)S(1)} %pad_add_fusion.place, bf16[2,6,256,128]{3,2,1,0:T(8,128)(2,1)S(1)} %get-tuple-element.103.padded, ...), custom_call_target="tpu_custom_call" | custom-call | flops 1207959552 | bytes 9568268 | tf_op jit(solution)/shard_map/pallas_call | solution.py:216
  113.5 2.6 %shard_map.82 = (bf16[2,6,256,128]{3,2,1,0:T(8,128)(2,1)S(1)}, bf16[2,6,256,128]{3,2,1,0:T(8,128)(2,1)S(1)}, bf16[2,2,256,128]{3,2,1,0:T(8,128)(2,1)S(1)}) custom-call(s32[3]{0:T(128)S(1)} %pad_add_fusion.place, bf16[2,2,256,128]{3,2,1,0:T(8,128)(2,1)S(1)} %broadcast_select_fusion.1.refs_0_.first, ...), custom_call_target="tpu_custom_call" | custom-call | flops 1207959552 | bytes 5242892 | tf_op jit(solution)/shard_map/pallas_call | solution.py:216
  116.5 3.5 %shard_map.83 = (bf16[3,256,768]{2,1,0:T(8,128)(2,1)S(1)}, bf16[3,256,768]{2,1,0:T(8,128)(2,1)S(1)}, bf16[3,256,768]{2,1,0:T(8,128)(2,1)}, f32[9,64,256]{2,1,0:T(8,128)S(1)}, f32[9,64,256]{2,1,0:T(8,128)S(1)}) custom-call(s32[3]{0:T(128)S(1)} %pad_add_fusion.place, bf16[2,6,256,128]{3,2,1,0:T(8,128)(2,1)S(1)} %get-tuple-element.93.padded, ...), custom_call_target="tpu_custom_call" | custom-call | flops 1207959552 | bytes 9568268 | tf_op jit(solution)/shard_map/pallas_call | solution.py:216
  122.0 1.6 %maximum_bitcast_fusion = bf16[1,4,1,256,2,128]{5,4,3,2,1,0:T(2,128)(2,1)} fusion(bf16[1,2,256,128]{3,1,2,0:T(2,128)(2,1)S(1)} %copy.33, bf16[2,2,256,128]{3,1,2,0:T(2,128)(2,1)S(1)} %copy.27, bf16[1,2,256,128]{3,1,2,0:T(2,128)(2,1)S(1)} %copy.32), kind=kLoop, calls=%fused_computation.2 | loop fusion | flops 524288 | bytes 1048576 | tf_op jit(solution)/shard_map/broadcast_in_dim | solution.py:331
  125.4 3.0 %shard_map.85 = (f32[2,9,64,256]{3,2,1,0:T(8,128)}, f32[2,9,64,256]{3,2,1,0:T(8,128)}) custom-call(s32[3]{0:T(128)S(1)} %pad_add_fusion.place, bf16[2,6,256,128]{3,2,1,0:T(8,128)(2,1)S(1)} %get-tuple-element.119.padded, bf16[2,2,256,128]{3,2,1,0:T(8,128)(2,1)S(1)} %collective-permute-done.38.refs_0_, ...), custom_call_target="tpu_custom_call" | custom-call | flops 1207959552 | bytes 4849676 | tf_op jit(solution)/shard_map/pallas_call | solution.py:216
  128.4 3.0 %shard_map.86 = (f32[2,9,64,256]{3,2,1,0:T(8,128)}, f32[2,9,64,256]{3,2,1,0:T(8,128)}) custom-call(s32[3]{0:T(128)S(1)} %pad_add_fusion.place, bf16[2,6,256,128]{3,2,1,0:T(8,128)(2,1)S(1)} %get-tuple-element.109.padded, bf16[2,2,256,128]{3,2,1,0:T(8,128)(2,1)S(1)} %collective-permute-done.39.refs_0_, ...), custom_call_target="tpu_custom_call", output_to_operand_aliasing={{0}: (6, {}), {1}: (7, {})} | custom-call | flops 1207959552 | bytes 7208972 | tf_op jit(solution)/shard_map/pallas_call | solution.py:216
  (112 shorter events, 37.7 us)
Async XLA Ops:
  3.4 19.0 %collective-permute-start.5 = (bf16[9,64,256]{2,1,0:T(8,128)(2,1)S(1)}, bf16[9,64,256]{2,1,0:T(8,128)(2,1)S(1)}, u32[]{:S(2)}, u32[]{:S(2)}) collective-permute-start(bf16[9,64,256]{2,1,0:T(8,128)(2,1)S(1)} %get-tuple-element.139.refs_0_), channel_id=1, source_target_pairs={{1,0},{0,1},{3,2},{2,3},{5,4},{4,5},{7,6},{6,7},{9,8},{8,9},{11,10... | collective-permute-start | bytes 884744 | tf_op jit(solution)/shard_map/ppermute | solution.py:29
  4.3 12.0 %collective-permute-start.3 = (bf16[9,64,256]{2,1,0:T(8,128)(2,1)S(1)}, bf16[9,64,256]{2,1,0:T(8,128)(2,1)S(1)}, u32[]{:S(2)}, u32[]{:S(2)}) collective-permute-start(bf16[9,64,256]{2,1,0:T(8,128)(2,1)S(1)} %get-tuple-element.140.refs_0_), channel_id=1, source_target_pairs={{2,0},{0,2},{3,1},{1,3},{6,4},{4,6},{7,5},{5,7},{10,8},{8,10},{11,... | collective-permute-start | bytes 884744 | tf_op jit(solution)/shard_map/ppermute | solution.py:29
  4.6 13.3 %collective-permute-start.2 = (bf16[9,64,256]{2,1,0:T(8,128)(2,1)S(1)}, bf16[9,64,256]{2,1,0:T(8,128)(2,1)S(1)}, u32[]{:S(2)}, u32[]{:S(2)}) collective-permute-start(bf16[9,64,256]{2,1,0:T(8,128)(2,1)S(1)} %get-tuple-element.140.refs_0_), channel_id=1, source_target_pairs={{1,0},{0,1},{3,2},{2,3},{5,4},{4,5},{7,6},{6,7},{9,8},{8,9},{11,10... | collective-permute-start | bytes 884744 | tf_op jit(solution)/shard_map/ppermute | solution.py:29
  6.1 18.6 %collective-permute-start.1 = (bf16[2,2,256,128]{3,2,1,0:T(8,128)(2,1)}, bf16[2,2,256,128]{3,2,1,0:T(8,128)(2,1)}, u32[]{:S(2)}, u32[]{:S(2)}) collective-permute-start(bf16[2,2,256,128]{3,2,1,0:T(8,128)(2,1)} %pad_maximum_fusion.1.refs_2_), channel_id=1, source_target_pairs={{1,0},{0,1},{3,2},{2,3},{5,4},{4,5},{7,6},{6,7},{9,8},{8,9},{11,10... | collective-permute-start | bytes 786440 | tf_op jit(solution)/shard_map/ppermute | solution.py:29
  10.0 15.9 %collective-permute-start = (bf16[2,2,256,128]{3,2,1,0:T(8,128)(2,1)S(1)}, bf16[2,2,256,128]{3,2,1,0:T(8,128)(2,1)}, u32[]{:S(2)}, u32[]{:S(2)}) collective-permute-start(bf16[2,2,256,128]{3,2,1,0:T(8,128)(2,1)S(1)} %pad_maximum_fusion.refs_0_.first), channel_id=1, source_target_pairs={{1,0},{0,1},{3,2},{2,3},{5,4},{4,5},{7,6},{6,7},{9,8},{8,9},{11,10... | collective-permute-start | bytes 786440 | tf_op jit(solution)/shard_map/ppermute | solution.py:29
  19.7 13.5 %collective-permute-start.12 = (bf16[2,2,256,128]{3,2,1,0:T(8,128)(2,1)S(1)}, bf16[2,2,256,128]{3,2,1,0:T(8,128)(2,1)S(1)}, u32[]{:S(2)}, u32[]{:S(2)}) collective-permute-start(bf16[2,2,256,128]{3,2,1,0:T(8,128)(2,1)S(1)} %pad_maximum_fusion.refs_0_.first), channel_id=1, source_target_pairs={{2,0},{0,2},{3,1},{1,3},{6,4},{4,6},{7,5},{5,7},{10,8},{8,10},{11,... | collective-permute-start | bytes 786440 | tf_op jit(solution)/shard_map/ppermute | solution.py:29
  22.4 13.8 %collective-permute-start.20 = (bf16[9,64,256]{2,1,0:T(8,128)(2,1)S(1)}, bf16[9,64,256]{2,1,0:T(8,128)(2,1)S(1)}, u32[]{:S(2)}, u32[]{:S(2)}) collective-permute-start(bf16[9,64,256]{2,1,0:T(8,128)(2,1)S(1)} %get-tuple-element.141.refs_0_), channel_id=1, source_target_pairs={{2,0},{0,2},{3,1},{1,3},{6,4},{4,6},{7,5},{5,7},{10,8},{8,10},{11,... | collective-permute-start | bytes 884744 | tf_op jit(solution)/shard_map/ppermute | solution.py:29
  22.7 20.2 %collective-permute-start.19 = (bf16[9,64,256]{2,1,0:T(8,128)(2,1)S(1)}, bf16[9,64,256]{2,1,0:T(8,128)(2,1)S(1)}, u32[]{:S(2)}, u32[]{:S(2)}) collective-permute-start(bf16[9,64,256]{2,1,0:T(8,128)(2,1)S(1)} %get-tuple-element.141.refs_0_), channel_id=1, source_target_pairs={{1,0},{0,1},{3,2},{2,3},{5,4},{4,5},{7,6},{6,7},{9,8},{8,9},{11,10... | collective-permute-start | bytes 884744 | tf_op jit(solution)/shard_map/ppermute | solution.py:29
  24.7 18.2 %collective-permute-start.15 = (bf16[9,64,256]{2,1,0:T(8,128)(2,1)S(1)}, bf16[9,64,256]{2,1,0:T(8,128)(2,1)S(1)}, u32[]{:S(2)}, u32[]{:S(2)}) collective-permute-start(bf16[9,64,256]{2,1,0:T(8,128)(2,1)S(1)} %get-tuple-element.142.refs_0_), channel_id=1, source_target_pairs={{2,0},{0,2},{3,1},{1,3},{6,4},{4,6},{7,5},{5,7},{10,8},{8,10},{11,... | collective-permute-start | bytes 884744 | tf_op jit(solution)/shard_map/ppermute | solution.py:29
  30.5 10.4 %collective-permute-start.8 = (bf16[2,2,256,128]{3,2,1,0:T(8,128)(2,1)S(1)}, bf16[2,2,256,128]{3,2,1,0:T(8,128)(2,1)S(1)}, u32[]{:S(2)}, u32[]{:S(2)}) collective-permute-start(bf16[2,2,256,128]{3,2,1,0:T(8,128)(2,1)S(1)} %shard_map.70), channel_id=1, source_target_pairs={{4,0},{8,4},{12,8},{16,12},{20,16},{24,20},{28,24},{5,1},{9,5},{13... | collective-permute-start | bytes 786440 | tf_op jit(solution)/shard_map/ppermute | solution.py:324
  33.1 13.4 %collective-permute-start.10 = (bf16[2,2,256,128]{3,2,1,0:T(8,128)(2,1)S(1)}, bf16[2,2,256,128]{3,2,1,0:T(8,128)(2,1)S(1)}, u32[]{:S(2)}, u32[]{:S(2)}) collective-permute-start(bf16[2,2,256,128]{3,2,1,0:T(8,128)(2,1)S(1)} %get-tuple-element.70.second), channel_id=1, source_target_pairs={{4,0},{8,4},{12,8},{16,12},{20,16},{24,20},{28,24},{5,1},{9,5},{13... | collective-permute-start | bytes 786440 | tf_op jit(solution)/shard_map/ppermute | solution.py:315
  36.2 10.6 %collective-permute-start.14 = (bf16[9,64,256]{2,1,0:T(8,128)(2,1)S(1)}, bf16[9,64,256]{2,1,0:T(8,128)(2,1)S(1)}, u32[]{:S(2)}, u32[]{:S(2)}) collective-permute-start(bf16[9,64,256]{2,1,0:T(8,128)(2,1)S(1)} %get-tuple-element.142.refs_0_), channel_id=1, source_target_pairs={{1,0},{0,1},{3,2},{2,3},{5,4},{4,5},{7,6},{6,7},{9,8},{8,9},{11,10... | collective-permute-start | bytes 884744 | tf_op jit(solution)/shard_map/ppermute | solution.py:29
  42.9 13.7 %collective-permute-start.13 = (bf16[2,2,256,128]{3,2,1,0:T(8,128)(2,1)S(1)}, bf16[2,2,256,128]{3,2,1,0:T(8,128)(2,1)S(1)}, u32[]{:S(2)}, u32[]{:S(2)}) collective-permute-start(bf16[2,2,256,128]{3,2,1,0:T(8,128)(2,1)S(1)} %collective-permute-done.12.refs_0_), channel_id=1, source_target_pairs={{1,0},{0,1},{3,2},{2,3},{5,4},{4,5},{7,6},{6,7},{9,8},{8,9},{11,10... | collective-permute-start | bytes 786440 | tf_op jit(solution)/shard_map/ppermute | solution.py:29
  42.9 12.9 %collective-permute-start.16 = (bf16[9,64,256]{2,1,0:T(8,128)(2,1)S(1)}, bf16[9,64,256]{2,1,0:T(8,128)(2,1)S(1)}, u32[]{:S(2)}, u32[]{:S(2)}) collective-permute-start(bf16[9,64,256]{2,1,0:T(8,128)(2,1)S(1)} %collective-permute-done.15.refs_2_), channel_id=1, source_target_pairs={{1,0},{0,1},{3,2},{2,3},{5,4},{4,5},{7,6},{6,7},{9,8},{8,9},{11,10... | collective-permute-start | bytes 884744 | tf_op jit(solution)/shard_map/ppermute | solution.py:29
  46.8 13.2 %collective-permute-start.11 = (bf16[2,2,256,128]{3,2,1,0:T(8,128)(2,1)S(1)}, bf16[2,2,256,128]{3,2,1,0:T(8,128)(2,1)S(1)}, u32[]{:S(2)}, u32[]{:S(2)}) collective-permute-start(bf16[2,2,256,128]{3,2,1,0:T(8,128)(2,1)S(1)} %broadcast_select_fusion.4.refs_2_), channel_id=1, source_target_pairs={{1,0},{0,1},{3,2},{2,3},{5,4},{4,5},{7,6},{6,7},{9,8},{8,9},{11,10... | collective-permute-start | bytes 786440 | tf_op jit(solution)/shard_map/ppermute | solution.py:29
  48.3 11.7 %collective-permute-start.9 = (bf16[2,2,256,128]{3,2,1,0:T(8,128)(2,1)S(1)}, bf16[2,2,256,128]{3,2,1,0:T(8,128)(2,1)S(1)}, u32[]{:S(2)}, u32[]{:S(2)}) collective-permute-start(bf16[2,2,256,128]{3,2,1,0:T(8,128)(2,1)S(1)} %broadcast_select_fusion.5.refs_0_.first), channel_id=1, source_target_pairs={{1,0},{0,1},{3,2},{2,3},{5,4},{4,5},{7,6},{6,7},{9,8},{8,9},{11,10... | collective-permute-start | bytes 786440 | tf_op jit(solution)/shard_map/ppermute | solution.py:29
  53.2 12.8 %collective-permute-start.18 = (bf16[2,2,256,128]{3,2,1,0:T(8,128)(2,1)S(1)}, bf16[2,2,256,128]{3,2,1,0:T(8,128)(2,1)S(1)}, u32[]{:S(2)}, u32[]{:S(2)}) collective-permute-start(bf16[2,2,256,128]{3,2,1,0:T(8,128)(2,1)S(1)} %collective-permute-done.17.refs_0_), channel_id=1, source_target_pairs={{1,0},{0,1},{3,2},{2,3},{5,4},{4,5},{7,6},{6,7},{9,8},{8,9},{11,10... | collective-permute-start | bytes 786440 | tf_op jit(solution)/shard_map/ppermute | solution.py:29
  59.7 14.0 %collective-permute-start.26 = (bf16[2,2,256,128]{3,2,1,0:T(8,128)(2,1)S(1)}, bf16[2,2,256,128]{3,2,1,0:T(8,128)(2,1)S(1)}, u32[]{:S(2)}, u32[]{:S(2)}) collective-permute-start(bf16[2,2,256,128]{3,2,1,0:T(8,128)(2,1)S(1)} %broadcast_select_fusion.5.refs_0_.first), channel_id=1, source_target_pairs={{2,0},{0,2},{3,1},{1,3},{6,4},{4,6},{7,5},{5,7},{10,8},{8,10},{11,... | collective-permute-start | bytes 786440 | tf_op jit(solution)/shard_map/ppermute | solution.py:29
  62.6 12.8 %collective-permute-start.28 = (bf16[2,2,256,128]{3,2,1,0:T(8,128)(2,1)S(1)}, bf16[2,2,256,128]{3,2,1,0:T(8,128)(2,1)S(1)}, u32[]{:S(2)}, u32[]{:S(2)}) collective-permute-start(bf16[2,2,256,128]{3,2,1,0:T(8,128)(2,1)S(1)} %get-tuple-element.80.second), channel_id=1, source_target_pairs={{2,0},{0,2},{3,1},{1,3},{6,4},{4,6},{7,5},{5,7},{10,8},{8,10},{11,... | collective-permute-start | bytes 786440 | tf_op jit(solution)/shard_map/ppermute | solution.py:29
  63.9 11.0 %collective-permute-start.24 = (bf16[2,2,256,128]{3,2,1,0:T(8,128)(2,1)S(1)}, bf16[2,2,256,128]{3,2,1,0:T(8,128)(2,1)S(1)}, u32[]{:S(2)}, u32[]{:S(2)}) collective-permute-start(bf16[2,2,256,128]{3,2,1,0:T(8,128)(2,1)S(1)} %get-tuple-element.80.second), channel_id=1, source_target_pairs={{4,0},{8,4},{12,8},{16,12},{20,16},{24,20},{28,24},{5,1},{9,5},{13... | collective-permute-start | bytes 786440 | tf_op jit(solution)/shard_map/ppermute | solution.py:315
  70.0 10.1 %collective-permute-start.22 = (bf16[2,2,256,128]{3,2,1,0:T(8,128)(2,1)S(1)}, bf16[2,2,256,128]{3,2,1,0:T(8,128)(2,1)S(1)}, u32[]{:S(2)}, u32[]{:S(2)}) collective-permute-start(bf16[2,2,256,128]{3,2,1,0:T(8,128)(2,1)S(1)} %shard_map.76), channel_id=1, source_target_pairs={{4,0},{8,4},{12,8},{16,12},{20,16},{24,20},{28,24},{5,1},{9,5},{13... | collective-permute-start | bytes 786440 | tf_op jit(solution)/shard_map/ppermute | solution.py:324
  73.7 8.2 %collective-permute-start.27 = (bf16[2,2,256,128]{3,2,1,0:T(8,128)(2,1)S(1)}, bf16[2,2,256,128]{3,2,1,0:T(8,128)(2,1)S(1)}, u32[]{:S(2)}, u32[]{:S(2)}) collective-permute-start(bf16[2,2,256,128]{3,2,1,0:T(8,128)(2,1)S(1)} %collective-permute-done.26.refs_0_), channel_id=1, source_target_pairs={{1,0},{0,1},{3,2},{2,3},{5,4},{4,5},{7,6},{6,7},{9,8},{8,9},{11,10... | collective-permute-start | bytes 786440 | tf_op jit(solution)/shard_map/ppermute | solution.py:29
  74.9 12.1 %collective-permute-start.25 = (bf16[2,2,256,128]{3,2,1,0:T(8,128)(2,1)S(1)}, bf16[2,2,256,128]{3,2,1,0:T(8,128)(2,1)S(1)}, u32[]{:S(2)}, u32[]{:S(2)}) collective-permute-start(bf16[2,2,256,128]{3,2,1,0:T(8,128)(2,1)S(1)} %broadcast_select_fusion.2.refs_2_), channel_id=1, source_target_pairs={{1,0},{0,1},{3,2},{2,3},{5,4},{4,5},{7,6},{6,7},{9,8},{8,9},{11,10... | collective-permute-start | bytes 786440 | tf_op jit(solution)/shard_map/ppermute | solution.py:29
  75.5 9.0 %collective-permute-start.29 = (bf16[2,2,256,128]{3,2,1,0:T(8,128)(2,1)S(1)}, bf16[2,2,256,128]{3,2,1,0:T(8,128)(2,1)S(1)}, u32[]{:S(2)}, u32[]{:S(2)}) collective-permute-start(bf16[2,2,256,128]{3,2,1,0:T(8,128)(2,1)S(1)} %collective-permute-done.28.refs_0_), channel_id=1, source_target_pairs={{1,0},{0,1},{3,2},{2,3},{5,4},{4,5},{7,6},{6,7},{9,8},{8,9},{11,10... | collective-permute-start | bytes 786440 | tf_op jit(solution)/shard_map/ppermute | solution.py:29
  81.6 16.5 %collective-permute-start.34 = (bf16[2,2,256,128]{3,2,1,0:T(8,128)(2,1)S(1)}, bf16[2,2,256,128]{3,2,1,0:T(8,128)(2,1)S(1)}, u32[]{:S(2)}, u32[]{:S(2)}) collective-permute-start(bf16[2,2,256,128]{3,2,1,0:T(8,128)(2,1)S(1)} %broadcast_select_fusion.3.refs_0_.first), channel_id=1, source_target_pairs={{2,0},{0,2},{3,1},{1,3},{6,4},{4,6},{7,5},{5,7},{10,8},{8,10},{11,... | collective-permute-start | bytes 786440 | tf_op jit(solution)/shard_map/ppermute | solution.py:29
  91.0 17.2 %collective-permute-start.30 = (bf16[2,2,256,128]{3,2,1,0:T(8,128)(2,1)S(1)}, bf16[2,2,256,128]{3,2,1,0:T(8,128)(2,1)S(1)}, u32[]{:S(2)}, u32[]{:S(2)}) collective-permute-start(bf16[2,2,256,128]{3,2,1,0:T(8,128)(2,1)S(1)} %shard_map.80), channel_id=1, source_target_pairs={{4,0},{8,4},{12,8},{16,12},{20,16},{24,20},{28,24},{5,1},{9,5},{13... | collective-permute-start | bytes 786440 | tf_op jit(solution)/shard_map/ppermute | solution.py:324
  93.4 15.0 %collective-permute-start.36 = (bf16[2,2,256,128]{3,2,1,0:T(8,128)(2,1)S(1)}, bf16[2,2,256,128]{3,2,1,0:T(8,128)(2,1)S(1)}, u32[]{:S(2)}, u32[]{:S(2)}) collective-permute-start(bf16[2,2,256,128]{3,2,1,0:T(8,128)(2,1)S(1)} %get-tuple-element.94.second), channel_id=1, source_target_pairs={{2,0},{0,2},{3,1},{1,3},{6,4},{4,6},{7,5},{5,7},{10,8},{8,10},{11,... | collective-permute-start | bytes 786440 | tf_op jit(solution)/shard_map/ppermute | solution.py:29
  94.6 12.3 %collective-permute-start.32 = (bf16[2,2,256,128]{3,2,1,0:T(8,128)(2,1)S(1)}, bf16[2,2,256,128]{3,2,1,0:T(8,128)(2,1)S(1)}, u32[]{:S(2)}, u32[]{:S(2)}) collective-permute-start(bf16[2,2,256,128]{3,2,1,0:T(8,128)(2,1)S(1)} %get-tuple-element.94.second), channel_id=1, source_target_pairs={{4,0},{8,4},{12,8},{16,12},{20,16},{24,20},{28,24},{5,1},{9,5},{13... | collective-permute-start | bytes 786440 | tf_op jit(solution)/shard_map/ppermute | solution.py:315
  98.1 11.9 %collective-permute-start.35 = (bf16[2,2,256,128]{3,2,1,0:T(8,128)(2,1)S(1)}, bf16[2,2,256,128]{3,2,1,0:T(8,128)(2,1)S(1)}, u32[]{:S(2)}, u32[]{:S(2)}) collective-permute-start(bf16[2,2,256,128]{3,2,1,0:T(8,128)(2,1)S(1)} %collective-permute-done.34.refs_0_), channel_id=1, source_target_pairs={{1,0},{0,1},{3,2},{2,3},{5,4},{4,5},{7,6},{6,7},{9,8},{8,9},{11,10... | collective-permute-start | bytes 786440 | tf_op jit(solution)/shard_map/ppermute | solution.py:29
  108.4 8.1 %collective-permute-start.37 = (bf16[2,2,256,128]{3,2,1,0:T(8,128)(2,1)S(1)}, bf16[2,2,256,128]{3,2,1,0:T(8,128)(2,1)S(1)}, u32[]{:S(2)}, u32[]{:S(2)}) collective-permute-start(bf16[2,2,256,128]{3,2,1,0:T(8,128)(2,1)S(1)} %collective-permute-done.36.refs_0_), channel_id=1, source_target_pairs={{1,0},{0,1},{3,2},{2,3},{5,4},{4,5},{7,6},{6,7},{9,8},{8,9},{11,10... | collective-permute-start | bytes 786440 | tf_op jit(solution)/shard_map/ppermute | solution.py:29
  108.9 14.7 %collective-permute-start.38 = (bf16[2,2,256,128]{3,2,1,0:T(8,128)(2,1)S(1)}, bf16[2,2,256,128]{3,2,1,0:T(8,128)(2,1)S(1)}, u32[]{:S(2)}, u32[]{:S(2)}) collective-permute-start(bf16[2,2,256,128]{3,2,1,0:T(8,128)(2,1)S(1)} %broadcast_select_fusion.1.refs_0_.first), channel_id=1, source_target_pairs={{2,0},{0,2},{3,1},{1,3},{6,4},{4,6},{7,5},{5,7},{10,8},{8,10},{11,... | collective-permute-start | bytes 786440 | tf_op jit(solution)/shard_map/ppermute | solution.py:29
  116.1 8.1 %collective-permute-start.39 = (bf16[2,2,256,128]{3,2,1,0:T(8,128)(2,1)S(1)}, bf16[2,2,256,128]{3,2,1,0:T(8,128)(2,1)S(1)}, u32[]{:S(2)}, u32[]{:S(2)}) collective-permute-start(bf16[2,2,256,128]{3,2,1,0:T(8,128)(2,1)S(1)} %get-tuple-element.110.second), channel_id=1, source_target_pairs={{2,0},{0,2},{3,1},{1,3},{6,4},{4,6},{7,5},{5,7},{10,8},{8,10},{11,... | collective-permute-start | bytes 786440 | tf_op jit(solution)/shard_map/ppermute | solution.py:29
  (14 other events, 65.3 us)

commit v2 on v1

--- a/solution.py
+++ b/solution.py
@@ -52,7 +52,11 @@
     stacked = jnp.concatenate(
         [jnp.concatenate([load(r + a) for r in range(count)], axis=1) for a in range(3)], axis=0
     )
-    sums = [jnp.dot(kernel[b], stacked, preferred_element_type=f32) for b in range(3)]
+    depth = kernel.shape[1]
+    joined = jnp.dot(
+        kernel[...].reshape(3 * depth, kernel.shape[2]), stacked, preferred_element_type=f32
+    )
+    sums = [joined[b * depth : (b + 1) * depth] for b in range(3)]
     width = stacked.shape[1] // count
     rows = []
     for r in range(count):
@@ -61,9 +65,11 @@
     return rows
 
 
-def stage_one(pieces, place, *refs):
+def stage_one(pieces, images, place, *refs):
     first, second = refs[:pieces], refs[pieces : 2 * pieces]
-    kernel, flip, padded_a, padded_b, own, raw, other = refs[2 * pieces :]
+    kernel, flip, padded_a, padded_b, own = refs[2 * pieces : 2 * pieces + 5]
+    packed = refs[2 * pieces + 5 : -2]
+    raw, other = refs[-2:]
     band = first[0].shape[1]
     rows = band * pieces
     zero = jnp.zeros(padded_a.shape[2:], bf16)
@@ -95,6 +101,13 @@
     for member in range(2):
         for r in range(band):
             own[member, r] = other[member, me * band + r]
+    channels = own.shape[2]
+    chunk = channels // images
+    for k, out in enumerate(packed):
+        goal = lax.rem(place[2] - (k + 1) + images, images)
+        for r in range(band):
+            out[r, :channels] = other[0, me * band + r]
+            out[r, channels:] = other[1, me * band + r, pl.ds(pl.multiple_of(goal * chunk, chunk), chunk), :]
 
 
 def stage_two(place, padded, first, second, kernel, flip, out):
@@ -109,16 +122,17 @@
         out[1, r] = (first[1, r].astype(f32) + slope * moved[r]).astype(bf16)
 
 
-def update(pieces, images, final, scale, place, padded, *refs):
+def update(pieces, images, final, keep_speed, scale, place, padded, *refs):
     count = pieces * (images - 1)
-    given, refs = refs[:count], refs[count:]
+    given, refs = refs[:count], list(refs[count:])
+    act, cot, total = refs[-3:]
     if final:
         params, moments = refs[:2]
-        params_out, moments_out, act, cot, moved = refs[-5:]
-        params_out, moments_out = params_out.at[0], moments_out.at[0]
+        params_out, moments_out = (ref.at[0] for ref in refs[-5:-3])
     else:
-        (weights, speed, params, moments, weights_out, flip_out, speed_out, params_out,
-         moments_out, act, cot, moved, total) = refs
+        weights, speed, params, moments, weights_out, flip_out = refs[:6]
+        speed_out = refs[6] if keep_speed else None
+        params_out, moments_out = refs[-5:-3]
     me, mine = place[0], place[1]
     if len(params.shape) == 4:
         params, moments = params.at[0], moments.at[0]
@@ -128,51 +142,63 @@
     part = params.shape[1]
     slot = pl.ds(pl.multiple_of(mine * part, part), part)
     kept = slot if final else slice(None)
+
+    def place_row(row, value):
+        cot[1, row] = value
+        value = value.astype(f32)
+        cot[0, row] = lane_shift(value, -1).astype(bf16)
+        cot[2, row] = lane_shift(value, 1).astype(bf16)
+
     for r in range(rows):
         act[r] = padded[0, r + 1]
-        cot[r] = padded[1, r + 1, kept, :]
+        place_row(r, padded[1, r + 1, kept, :])
     for image in range(images - 1):
         for s in range(pieces):
             piece = given[image * pieces + s]
             start = (image + 1) * rows + lax.rem(me + s, pieces) * band
             for r in range(band):
-                act[start + r] = silu16(piece[0, r])
-                cot[start + r] = piece[1, r, kept, :]
-    for b in range(3):
-        source = cot
-        if b != 1:
-            source = moved
-            for r in range(images * rows):
-                moved[r] = lane_shift(cot[r].astype(f32), b - 1).astype(bf16)
-        for a in range(3):
-            valid = [
-                (i * rows + r, i * rows + r + a - 1)
-                for i in range(images)
-                for r in range(rows)
-                if 0 <= r + a - 1 < rows
-            ]
-            left = jnp.concatenate([source[r] for r, _ in valid], axis=1)
-            right = jnp.concatenate([act[r] for _, r in valid], axis=1)
-            grad = lax.dot_general(
-                left, right, (((1,), (1,)), ((), ())), preferred_element_type=f32
-            )
+                if len(piece.shape) == 3:
+                    act[start + r] = silu16(piece[r, :channels])
+                    near = pl.ds(pl.multiple_of(channels + me * part, part), part)
+                    place_row(start + r, piece[r, near, :])
+                else:
+                    act[start + r] = silu16(piece[0, r])
+                    place_row(start + r, piece[1, r, kept, :])
+    depth = cot.shape[2]
+    for a in range(3):
+        valid = [
+            (i * rows + r, i * rows + r + a - 1)
+            for i in range(images)
+            for r in range(rows)
+            if 0 <= r + a - 1 < rows
+        ]
+        left = jnp.concatenate(
+            [jnp.concatenate([cot[b, r] for r, _ in valid], axis=1) for b in range(3)], axis=0
+        )
+        right = jnp.concatenate([act[r] for _, r in valid], axis=1)
+        total[...] = lax.dot_general(
+            left, right, (((1,), (1,)), ((), ())), preferred_element_type=f32
+        )
+        for b in range(3):
             tap = 3 * a + b
             if final:
-                mine_grad = grad
+                mine_grad = total[b * depth : (b + 1) * depth, :]
             else:
-                total[...] = grad
-                mine_grad = total[slot, :]
+                mine_grad = total[pl.ds(pl.multiple_of(b * depth + mine * part, part), part), :]
             step = momentum_decay * moments[tap] + scale * mine_grad
             moments_out[tap] = step
             params_out[tap] = params[tap] - learn_rate * step
             if not final:
                 cols = slice(a * channels, (a + 1) * channels)
+                grad = total[b * depth : (b + 1) * depth, :]
                 step = momentum_decay * speed[b, :, cols].astype(f32) + scale * grad
-                speed_out[b, :, cols] = step.astype(bf16)
+                if keep_speed:
+                    speed_out[b, :, cols] = step.astype(bf16)
                 fresh = weights[b, :, cols].astype(f32) - (learn_rate * scale) * step
-                weights_out[b, :, cols] = fresh.astype(bf16)
+                fresh = fresh.astype(bf16)
+                weights_out[b, :, cols] = fresh
                 back = slice((2 - a) * channels, (3 - a) * channels)
-                flip_out[2 - b, :, back] = fresh.T.astype(bf16)
+                flip_out[2 - b, :, back] = fresh.T
 
 
 def assemble(sections, pieces, flipping, place, *refs):
@@ -192,8 +218,8 @@
         flip = refs[count + 1]
         for a in range(3):
             for b in range(3):
-                block = out[b, :, a * channels : (a + 1) * channels].astype(f32)
-                flip[2 - b, :, (2 - a) * channels : (3 - a) * channels] = block.T.astype(bf16)
+                block = out[b, :, a * channels : (a + 1) * channels]
+                flip[2 - b, :, (2 - a) * channels : (3 - a) * channels] = block.T
 
 
 def call(body, outs, inputs, flops, scratch=(), slot=None, aliases=0, read=None):
@@ -220,7 +246,7 @@
         out_specs=out_specs,
         scratch_shapes=list(scratch),
         input_output_aliases=in_out,
-        compiler_params=pltpu.CompilerParams(vmem_limit_bytes=32 * 1024 * 1024),
+        compiler_params=pltpu.CompilerParams(vmem_limit_bytes=(8 + 4 * lax.axis_size("dp")) << 20),
         cost_estimate=pl.CostEstimate(flops=flops, bytes_accessed=size, transcendentals=0),
         **extra,
     )(*inputs)
@@ -256,39 +282,49 @@
         body = functools.partial(assemble, images, pieces, flipping)
         return call(body, [block] * (2 if flipping else 1), [place] + parts, channels**3)
 
-    def one(first, second, kernel, flip):
+    def one(first, second, kernel, flip, final):
         inputs = [place] + first + second + [kernel, flip]
         scratch = [pltpu.VMEM((rows, channels, width), bf16), pltpu.VMEM((2, rows, channels, width), bf16)]
-        return call(
-            functools.partial(stage_one, pieces), [padded, padded, message], inputs, conv_flops, scratch
-        )
+        outs = [padded, padded, message]
+        if final:
+            outs += [shape((band, channels + channels // images, width), bf16)] * (images - 1)
+        body = functools.partial(stage_one, pieces, images)
+        return call(body, outs, inputs, conv_flops, scratch)
 
     def two(padded_b, first, second, kernel, flip):
         inputs = [place, padded_b, first, second, kernel, flip]
         return call(stage_two, [message], inputs, conv_flops // pieces)[0]
 
-    def learn(padded_own, others, state, slot=None, pair=(), read=None):
+    def learn(padded_own, others, state, slot=None, pair=(), read=None, keep_speed=True):
         weights, speed, own_params, own_moments = state
         final = slot is not None
         share = own_params.shape[-2]
-        depths = (channels, share, share) if final else (channels,) * 3
-        scratch = [pltpu.VMEM((images * rows, depth, width), bf16) for depth in depths]
+        depth = share if final else channels
+        count = images * rows
+        scratch = [
+            pltpu.VMEM((count, channels, width), bf16),
+            pltpu.VMEM((3, count, depth, width), bf16),
+            pltpu.VMEM((3 * depth, channels), f32),
+        ]
         inputs = [place, padded_own] + others
         if final:
             outs = [shape((2,) + own_params.shape, f32)] * 2
             inputs += [own_params, own_moments, *pair]
         else:
             inputs += [weights, speed, own_params, own_moments]
-            outs = [block] * 3 + [shape(own_params.shape[-3:], f32)] * 2
-            scratch += [pltpu.VMEM((channels, channels), f32)]
-        body = functools.partial(update, pieces, images, final, scale)
+            outs = [block] * (3 if keep_speed else 2) + [shape(own_params.shape[-3:], f32)] * 2
+        body = functools.partial(update, pieces, images, final, keep_speed, scale)
         flops = 2 * 9 * channels * channels * rows * width * images
-        return call(body, outs, inputs, flops, scratch, slot, len(pair), read)
+        results = call(body, outs, inputs, flops, scratch, slot, len(pair), read)
+        if final or keep_speed:
+            return results
+        return [*results[:2], None, *results[2:]]
 
     kernel_g = (params[0, 1] * scale).astype(bf16)
     far_g = abroad(kernel_g)
     own_g = around(kernel_g, "spatial")
-    kernel_f = (params[0, 0] * scale).astype(bf16)
+    later_params, _ = lax.optimization_barrier((params, kernel_g))
+    kernel_f = (later_params[0, 0] * scale).astype(bf16)
     far_f = abroad(kernel_f)
     own_f = around(kernel_f, "spatial")
     first = rowwise(inbox[0], (0, 3))
@@ -310,10 +346,15 @@
     down = [(i, i - 1) for i in range(1, sections)]
     for tick in range(ticks):
         final = tick == ticks - 1
-        padded_a, padded_b, middle = one(first_all, second_all, weights_g, flip_g)
+        padded_a, padded_b, middle, *packed = one(first_all, second_all, weights_g, flip_g, final)
         if not final:
             second = lax.ppermute(middle, "section", down)
-        far_b = abroad(middle)
+        if final:
+            far_b = [
+                lax.ppermute(p, "dp", ring("dp", k + 1)) for k, p in enumerate(packed)
+            ]
+        else:
+            far_b = abroad(middle)
         if tick == 1:
             held, _ = lax.optimization_barrier((held, middle))
             weights_f, flip_f, speed_f, params_f, moments_f = learn(
@@ -330,7 +371,7 @@
             sent = jnp.stack([last[0], middle[0], middle[1], last[1]])
             outbox = jnp.swapaxes(sent, 1, 2)[None, :, None]
             outbox = with_layout_constraint(outbox, Layout(tuple(range(outbox.ndim))))
-            outbox, far_a = lax.optimization_barrier((outbox, far_a))
+            outbox, padded_a = lax.optimization_barrier((outbox, padded_a))
         others_g = spread(far_a)
         if tick == 0:
             far_mg = spread(far_mg)
@@ -342,7 +383,8 @@
             pair = learn(padded_a, others_g, state_g, 1)
         else:
             weights_g, flip_g, speed_g, params_g, moments_g = learn(
-                padded_a, others_g, state_g, read=1 if tick == 0 else None
+                padded_a, others_g, state_g, read=1 if tick == 0 else None,
+                keep_speed=tick < ticks - 2,
             )
         if not final:
             second = jnp.where(top_section, later[1], second)
@@ -363,7 +405,9 @@
             params_out, moments_out = learn(padded_b, others_f, state_f, 0, pair)
         else:
             state_f = (weights_f, speed_f, params_f, moments_f)
-            weights_f, flip_f, speed_f, params_f, moments_f = learn(padded_b, others_f, state_f)
+            weights_f, flip_f, speed_f, params_f, moments_f = learn(
+                padded_b, others_f, state_f, keep_speed=tick < ticks - 2
+            )
     return outbox, params_out[None], moments_out[None]
 
 

time: 132 us -> 130 us (0.985)
  Pallas kernels: 43.5 us -> 40.1 us
    pallas_call x20, Pallas kernels: 43.5 us -> 40.1 us  [call(): pl.pallas_call(body, out_shape=outs, in_specs=in_specs, out_specs=out_spe...]
    ppermute x36 -> x35, waiting for transfers between devices: 12.1 us -> 11.7 us  [around(): lax.ppermute(shard, axis, ring(axis, k))]
    ppermute x36 -> x35, starting transfers between devices: 30.7 us -> 30.6 us  [around(): lax.ppermute(shard, axis, ring(axis, k))]
  transfers between devices with their start and end apart: 42 -> 42, of which waited for: 9 -> 9; matrix products, arithmetic and copies ran while one was open for 5% -> 5% of each run, Pallas kernels for 31% -> 29%
where the time goes in v2:
time: 130 us
  starting transfers between devices  46.8 us (36%)
  Pallas kernels  40.1 us (31%)
  waiting for transfers between devices  31.4 us (24%)
  other arithmetic  5.94 us (5%)
  local copies, waits for them, and re-layouts  3.99 us (3%)
    pallas_call x20, Pallas kernels, call(): pl.pallas_call(body, out_shape=outs, in_specs=in_specs, out_specs=out_spe...  40.1 us
    ppermute x35, starting transfers between devices, around(): lax.ppermute(shard, axis, ring(axis, k))  30.6 us
    ppermute x35, waiting for transfers between devices, around(): lax.ppermute(shard, axis, ring(axis, k))  11.7 us
    ppermute x3, waiting for transfers between devices, local(): second = lax.ppermute(middle, 'section', down)  10.7 us
    ppermute x3, waiting for transfers between devices, local(): following = lax.ppermute(last, 'section', down)  8.46 us
    ppermute x3, starting transfers between devices, local(): second = lax.ppermute(middle, 'section', down)  8.16 us
    ppermute x3, starting transfers between devices, local(): following = lax.ppermute(last, 'section', down)  7.72 us
  transfers between devices with their start and end apart: 42, of which 9 were waited for; matrix products, arithmetic and copies ran while one was open for 5% of the time, Pallas kernels for 29%

profile of v2, /device:TPU:21, one launch (start us, length us, event | category | flops | bytes accessed | tf_op | source)
XLA Modules:
  0.0 129.5 jit_solution(124525571903284209)
XLA Ops:
  8.3 2.6 %collective-permute-done.6.refs_2_ = bf16[9,64,256]{2,1,0:T(8,128)(2,1)S(1)} collective-permute-done((bf16[9,64,256]{2,1,0:T(8,128)(2,1)S(1)}, bf16[9,64,256]{2,1,0:T(8,128)(2,1)S(1)}, u32[]{:S(2)}, u32[]{:S(2)}) %collective-permute-start.6) | collective-permute-done | bytes 294944 | tf_op jit(solution)/shard_map/ppermute | solution.py:29
  10.9 2.7 %collective-permute-start = (bf16[2,2,256,128]{3,2,1,0:T(8,128)(2,1)S(1)}, bf16[2,2,256,128]{3,2,1,0:T(8,128)(2,1)}, u32[]{:S(2)}, u32[]{:S(2)}) collective-permute-start(bf16[2,2,256,128]{3,2,1,0:T(8,128)(2,1)S(1)} %pad_maximum_fusion.refs_0_.first), channel_id=1, source_target_pairs={{1,0},{0,1},{3,2},{2,3},{5,4},{4,5},{7,6},{6,7},{9,8},{8,9},{11,10... | collective-permute-start | bytes 786440 | tf_op jit(solution)/shard_map/ppermute | solution.py:29
  13.6 3.7 %collective-permute-done.3.refs_2_ = bf16[9,64,256]{2,1,0:T(8,128)(2,1)S(1)} collective-permute-done((bf16[9,64,256]{2,1,0:T(8,128)(2,1)S(1)}, bf16[9,64,256]{2,1,0:T(8,128)(2,1)S(1)}, u32[]{:S(2)}, u32[]{:S(2)}) %collective-permute-start.3) | collective-permute-done | bytes 294944 | tf_op jit(solution)/shard_map/ppermute | solution.py:29
  17.2 1.5 %collective-permute-start.7 = (bf16[9,64,256]{2,1,0:T(8,128)(2,1)S(1)}, bf16[9,64,256]{2,1,0:T(8,128)(2,1)S(1)}, u32[]{:S(2)}, u32[]{:S(2)}) collective-permute-start(bf16[9,64,256]{2,1,0:T(8,128)(2,1)S(1)} %collective-permute-done.6.refs_2_), channel_id=1, source_target_pairs={{1,0},{0,1},{3,2},{2,3},{5,4},{4,5},{7,6},{6,7},{9,8},{8,9},{11,10... | collective-permute-start | bytes 884744 | tf_op jit(solution)/shard_map/ppermute | solution.py:29
  26.7 3.1 %shard_map.68 = (bf16[2,6,256,128]{3,2,1,0:T(8,128)(2,1)S(1)}, bf16[2,6,256,128]{3,2,1,0:T(8,128)(2,1)S(1)}, bf16[2,2,256,128]{3,2,1,0:T(8,128)(2,1)S(1)}) custom-call(s32[3]{0:T(128)S(1)} %pad_add_fusion.place, bf16[2,2,256,128]{3,2,1,0:T(8,128)(2,1)S(1)} %pad_maximum_fusion.refs_0_.first, bf16[2,2,256,128]{3,2,1,0:T(8,128)(2,1)} %collective-permute-done.refs_1_, ...), custom_call_target="tpu_custom_call" | custom-call | flops 1207959552 | bytes 5242892 | tf_op jit(solution)/shard_map/pallas_call | solution.py:242
  29.8 1.5 %shard_map.70 = bf16[2,2,256,128]{3,2,1,0:T(8,128)(2,1)S(1)} custom-call(s32[3]{0:T(128)S(1)} %pad_add_fusion.place, bf16[2,6,256,128]{3,2,1,0:T(8,128)(2,1)S(1)} %get-tuple-element.84.padded, bf16[2,2,256,128]{3,2,1,0:T(8,128)(2,1)S(1)} %pad_maximum_fusion.refs_0_.first, bf16[2,2,256,128]{3,2,1,0:T(8,128)(2,1)S(1)} %get-tuple-element.72.second, ...), custom_call_target="tpu_custom_call" | custom-call | flops 603979776 | bytes 3932172 | tf_op jit(solution)/shard_map/pallas_call | solution.py:242
  31.3 2.1 %collective-permute-start.8 = (bf16[2,2,256,128]{3,2,1,0:T(8,128)(2,1)S(1)}, bf16[2,2,256,128]{3,2,1,0:T(8,128)(2,1)S(1)}, u32[]{:S(2)}, u32[]{:S(2)}) collective-permute-start(bf16[2,2,256,128]{3,2,1,0:T(8,128)(2,1)S(1)} %shard_map.70), channel_id=1, source_target_pairs={{4,0},{8,4},{12,8},{16,12},{20,16},{24,20},{28,24},{5,1},{9,5},{13... | collective-permute-start | bytes 786440 | tf_op jit(solution)/shard_map/ppermute | solution.py:365
  33.9 3.0 %collective-permute-start.10 = (bf16[2,2,256,128]{3,2,1,0:T(8,128)(2,1)S(1)}, bf16[2,2,256,128]{3,2,1,0:T(8,128)(2,1)S(1)}, u32[]{:S(2)}, u32[]{:S(2)}) collective-permute-start(bf16[2,2,256,128]{3,2,1,0:T(8,128)(2,1)S(1)} %get-tuple-element.72.second), channel_id=1, source_target_pairs={{4,0},{8,4},{12,8},{16,12},{20,16},{24,20},{28,24},{5,1},{9,5},{13... | collective-permute-start | bytes 786440 | tf_op jit(solution)/shard_map/ppermute | solution.py:351
  37.9 3.8 %collective-permute-done.8 = bf16[2,2,256,128]{3,2,1,0:T(8,128)(2,1)S(1)} collective-permute-done((bf16[2,2,256,128]{3,2,1,0:T(8,128)(2,1)S(1)}, bf16[2,2,256,128]{3,2,1,0:T(8,128)(2,1)S(1)}, u32[]{:S(2)}, u32[]{:S(2)}) %collective-permute-start.8) | collective-permute-done | bytes 262176 | tf_op jit(solution)/shard_map/ppermute | solution.py:365
  41.7 1.9 %collective-permute-start.21 = (bf16[9,64,256]{2,1,0:T(8,128)(2,1)S(1)}, bf16[9,64,256]{2,1,0:T(8,128)(2,1)S(1)}, u32[]{:S(2)}, u32[]{:S(2)}) collective-permute-start(bf16[9,64,256]{2,1,0:T(8,128)(2,1)S(1)} %collective-permute-done.20.refs_2_), channel_id=1, source_target_pairs={{1,0},{0,1},{3,2},{2,3},{5,4},{4,5},{7,6},{6,7},{9,8},{8,9},{11,10... | collective-permute-start | bytes 884744 | tf_op jit(solution)/shard_map/ppermute | solution.py:29
  44.2 3.1 %collective-permute-done.10 = bf16[2,2,256,128]{3,2,1,0:T(8,128)(2,1)S(1)} collective-permute-done((bf16[2,2,256,128]{3,2,1,0:T(8,128)(2,1)S(1)}, bf16[2,2,256,128]{3,2,1,0:T(8,128)(2,1)S(1)}, u32[]{:S(2)}, u32[]{:S(2)}) %collective-permute-start.10) | collective-permute-done | bytes 262176 | tf_op jit(solution)/shard_map/ppermute | solution.py:351
  49.2 4.8 %collective-permute-done.17.refs_0_ = bf16[2,2,256,128]{3,2,1,0:T(8,128)(2,1)S(1)} collective-permute-done((bf16[2,2,256,128]{3,2,1,0:T(8,128)(2,1)S(1)}, bf16[2,2,256,128]{3,2,1,0:T(8,128)(2,1)S(1)}, u32[]{:S(2)}, u32[]{:S(2)}) %collective-permute-start.17) | collective-permute-done | bytes 262176 | tf_op jit(solution)/shard_map/ppermute | solution.py:29
  54.0 2.0 %collective-permute-start.18 = (bf16[2,2,256,128]{3,2,1,0:T(8,128)(2,1)S(1)}, bf16[2,2,256,128]{3,2,1,0:T(8,128)(2,1)S(1)}, u32[]{:S(2)}, u32[]{:S(2)}) collective-permute-start(bf16[2,2,256,128]{3,2,1,0:T(8,128)(2,1)S(1)} %collective-permute-done.17.refs_0_), channel_id=1, source_target_pairs={{1,0},{0,1},{3,2},{2,3},{5,4},{4,5},{7,6},{6,7},{9,8},{8,9},{11,10... | collective-permute-start | bytes 786440 | tf_op jit(solution)/shard_map/ppermute | solution.py:29
  57.9 2.6 %shard_map.72 = (bf16[3,256,768]{2,1,0:T(8,128)(2,1)S(1)}, bf16[3,256,768]{2,1,0:T(8,128)(2,1)S(1)}, bf16[3,256,768]{2,1,0:T(8,128)(2,1)S(1)}, f32[9,64,256]{2,1,0:T(8,128)S(1)}, f32[9,64,256]{2,1,0:T(8,128)S(1)}) custom-call(s32[3]{0:T(128)S(1)} %pad_add_fusion.place, bf16[2,6,256,128]{3,2,1,0:T(8,128)(2,1)S(1)} %get-tuple-element.79.padded, ...), custom_call_target="tpu_custom_call" | custom-call | flops 1207959552 | bytes 10747916 | tf_op jit(solution)/shard_map/pallas_call | solution.py:242
  60.9 2.5 %shard_map.73 = (bf16[2,6,256,128]{3,2,1,0:T(8,128)(2,1)S(1)}, bf16[2,6,256,128]{3,2,1,0:T(8,128)(2,1)S(1)}, bf16[2,2,256,128]{3,2,1,0:T(8,128)(2,1)S(1)}) custom-call(s32[3]{0:T(128)S(1)} %pad_add_fusion.place, bf16[2,2,256,128]{3,2,1,0:T(8,128)(2,1)S(1)} %broadcast_select_fusion.5.refs_0_.first, ...), custom_call_target="tpu_custom_call" | custom-call | flops 1207959552 | bytes 5242892 | tf_op jit(solution)/shard_map/pallas_call | solution.py:242
  64.6 2.1 %collective-permute-start.24 = (bf16[2,2,256,128]{3,2,1,0:T(8,128)(2,1)S(1)}, bf16[2,2,256,128]{3,2,1,0:T(8,128)(2,1)S(1)}, u32[]{:S(2)}, u32[]{:S(2)}) collective-permute-start(bf16[2,2,256,128]{3,2,1,0:T(8,128)(2,1)S(1)} %get-tuple-element.83.second), channel_id=1, source_target_pairs={{4,0},{8,4},{12,8},{16,12},{20,16},{24,20},{28,24},{5,1},{9,5},{13... | collective-permute-start | bytes 786440 | tf_op jit(solution)/shard_map/ppermute | solution.py:351
  66.7 2.6 %shard_map.75 = (bf16[3,256,768]{2,1,0:T(8,128)(2,1)S(1)}, bf16[3,256,768]{2,1,0:T(8,128)(2,1)S(1)}, bf16[3,256,768]{2,1,0:T(8,128)(2,1)S(1)}, f32[9,64,256]{2,1,0:T(8,128)S(1)}, f32[9,64,256]{2,1,0:T(8,128)S(1)}) custom-call(s32[3]{0:T(128)S(1)} %pad_add_fusion.place, bf16[2,6,256,128]{3,2,1,0:T(8,128)(2,1)S(1)} %get-tuple-element.84.padded, ...), custom_call_target="tpu_custom_call" | custom-call | flops 1207959552 | bytes 10747916 | tf_op jit(solution)/shard_map/pallas_call | solution.py:242
  70.8 3.3 %collective-permute-start.22 = (bf16[2,2,256,128]{3,2,1,0:T(8,128)(2,1)S(1)}, bf16[2,2,256,128]{3,2,1,0:T(8,128)(2,1)S(1)}, u32[]{:S(2)}, u32[]{:S(2)}) collective-permute-start(bf16[2,2,256,128]{3,2,1,0:T(8,128)(2,1)S(1)} %shard_map.76), channel_id=1, source_target_pairs={{4,0},{8,4},{12,8},{16,12},{20,16},{24,20},{28,24},{5,1},{9,5},{13... | collective-permute-start | bytes 786440 | tf_op jit(solution)/shard_map/ppermute | solution.py:365
  76.3 4.6 %collective-permute-done.22 = bf16[2,2,256,128]{3,2,1,0:T(8,128)(2,1)S(1)} collective-permute-done((bf16[2,2,256,128]{3,2,1,0:T(8,128)(2,1)S(1)}, bf16[2,2,256,128]{3,2,1,0:T(8,128)(2,1)S(1)}, u32[]{:S(2)}, u32[]{:S(2)}) %collective-permute-start.22) | collective-permute-done | bytes 262176 | tf_op jit(solution)/shard_map/ppermute | solution.py:365
  82.7 2.6 %shard_map.77 = (bf16[3,256,768]{2,1,0:T(8,128)(2,1)S(1)}, bf16[3,256,768]{2,1,0:T(8,128)(2,1)S(1)}, bf16[3,256,768]{2,1,0:T(8,128)(2,1)S(1)}, f32[9,64,256]{2,1,0:T(8,128)S(1)}, f32[9,64,256]{2,1,0:T(8,128)S(1)}) custom-call(s32[3]{0:T(128)S(1)} %pad_add_fusion.place, bf16[2,6,256,128]{3,2,1,0:T(8,128)(2,1)S(1)} %get-tuple-element.90.padded, ...), custom_call_target="tpu_custom_call" | custom-call | flops 1207959552 | bytes 9568268 | tf_op jit(solution)/shard_map/pallas_call | solution.py:242
  85.3 2.6 %shard_map.79 = (bf16[3,256,768]{2,1,0:T(8,128)(2,1)S(1)}, bf16[3,256,768]{2,1,0:T(8,128)(2,1)S(1)}, bf16[3,256,768]{2,1,0:T(8,128)(2,1)S(1)}, f32[9,64,256]{2,1,0:T(8,128)S(1)}, f32[9,64,256]{2,1,0:T(8,128)S(1)}) custom-call(s32[3]{0:T(128)S(1)} %pad_add_fusion.place, bf16[2,6,256,128]{3,2,1,0:T(8,128)(2,1)S(1)} %get-tuple-element.82.padded, ...), custom_call_target="tpu_custom_call" | custom-call | flops 1207959552 | bytes 9568268 | tf_op jit(solution)/shard_map/pallas_call | solution.py:242
  87.9 2.5 %shard_map.78 = (bf16[2,6,256,128]{3,2,1,0:T(8,128)(2,1)S(1)}, bf16[2,6,256,128]{3,2,1,0:T(8,128)(2,1)S(1)}, bf16[2,2,256,128]{3,2,1,0:T(8,128)(2,1)S(1)}) custom-call(s32[3]{0:T(128)S(1)} %pad_add_fusion.place, bf16[2,2,256,128]{3,2,1,0:T(8,128)(2,1)S(1)} %broadcast_select_fusion.3.refs_0_.first, ...), custom_call_target="tpu_custom_call" | custom-call | flops 1207959552 | bytes 5242892 | tf_op jit(solution)/shard_map/pallas_call | solution.py:242
  91.9 2.3 %collective-permute-start.30 = (bf16[2,2,256,128]{3,2,1,0:T(8,128)(2,1)S(1)}, bf16[2,2,256,128]{3,2,1,0:T(8,128)(2,1)S(1)}, u32[]{:S(2)}, u32[]{:S(2)}) collective-permute-start(bf16[2,2,256,128]{3,2,1,0:T(8,128)(2,1)S(1)} %shard_map.80), channel_id=1, source_target_pairs={{4,0},{8,4},{12,8},{16,12},{20,16},{24,20},{28,24},{5,1},{9,5},{13... | collective-permute-start | bytes 786440 | tf_op jit(solution)/shard_map/ppermute | solution.py:365
  95.5 3.0 %collective-permute-start.32 = (bf16[2,2,256,128]{3,2,1,0:T(8,128)(2,1)S(1)}, bf16[2,2,256,128]{3,2,1,0:T(8,128)(2,1)S(1)}, u32[]{:S(2)}, u32[]{:S(2)}) collective-permute-start(bf16[2,2,256,128]{3,2,1,0:T(8,128)(2,1)S(1)} %get-tuple-element.97.second), channel_id=1, source_target_pairs={{4,0},{8,4},{12,8},{16,12},{20,16},{24,20},{28,24},{5,1},{9,5},{13... | collective-permute-start | bytes 786440 | tf_op jit(solution)/shard_map/ppermute | solution.py:351
  100.2 7.6 %collective-permute-done.32 = bf16[2,2,256,128]{3,2,1,0:T(8,128)(2,1)S(1)} collective-permute-done((bf16[2,2,256,128]{3,2,1,0:T(8,128)(2,1)S(1)}, bf16[2,2,256,128]{3,2,1,0:T(8,128)(2,1)S(1)}, u32[]{:S(2)}, u32[]{:S(2)}) %collective-permute-start.32) | collective-permute-done | bytes 262176 | tf_op jit(solution)/shard_map/ppermute | solution.py:351
  110.9 2.6 %shard_map.81 = (bf16[3,256,768]{2,1,0:T(8,128)(2,1)S(1)}, bf16[3,256,768]{2,1,0:T(8,128)(2,1)S(1)}, f32[9,64,256]{2,1,0:T(8,128)S(1)}, f32[9,64,256]{2,1,0:T(8,128)S(1)}) custom-call(s32[3]{0:T(128)S(1)} %pad_add_fusion.place, bf16[2,6,256,128]{3,2,1,0:T(8,128)(2,1)S(1)} %get-tuple-element.106.padded, ...), custom_call_target="tpu_custom_call" | custom-call | flops 1207959552 | bytes 8388620 | tf_op jit(solution)/shard_map/pallas_call | solution.py:242
  113.5 2.5 %shard_map.82 = (bf16[2,6,256,128]{3,2,1,0:T(8,128)(2,1)S(1)}, bf16[2,6,256,128]{3,2,1,0:T(8,128)(2,1)S(1)}, bf16[2,2,256,128]{3,2,1,0:T(8,128)(2,1)S(1)}, bf16[2,384,128]{2,1,0:T(8,128)(2,1)S(1)}) custom-call(s32[3]{0:T(128)S(1)} %pad_add_fusion.place, bf16[2,2,256,128]{3,2,1,0:T(8,128)(2,1)S(1)} %broadcast_select_fusion.1.refs_0_.first, ...), custom_call_target="tpu_custom_call" | custom-call | flops 1207959552 | bytes 5439500 | tf_op jit(solution)/shard_map/pallas_call | solution.py:242
  116.6 2.6 %shard_map.83 = (bf16[3,256,768]{2,1,0:T(8,128)(2,1)S(1)}, bf16[3,256,768]{2,1,0:T(8,128)(2,1)S(1)}, f32[9,64,256]{2,1,0:T(8,128)S(1)}, f32[9,64,256]{2,1,0:T(8,128)S(1)}) custom-call(s32[3]{0:T(128)S(1)} %pad_add_fusion.place, bf16[2,6,256,128]{3,2,1,0:T(8,128)(2,1)S(1)} %get-tuple-element.96.padded, ...), custom_call_target="tpu_custom_call" | custom-call | flops 1207959552 | bytes 8388620 | tf_op jit(solution)/shard_map/pallas_call | solution.py:242
  119.2 1.5 %shard_map.84 = bf16[2,2,256,128]{3,2,1,0:T(8,128)(2,1)S(1)} custom-call(s32[3]{0:T(128)S(1)} %pad_add_fusion.place, bf16[2,6,256,128]{3,2,1,0:T(8,128)(2,1)S(1)} %get-tuple-element.112.padded, bf16[2,2,256,128]{3,2,1,0:T(8,128)(2,1)S(1)} %broadcast_select_fusion.1.refs_0_.first, bf16[2,2,256,128]{3,2,1,0:T(8,128)(2,1)S(1)} %get-tuple-element.113.second, ...), custom_call_target="tpu_custom_call" | custom-call | flops 603979776 | bytes 3932172 | tf_op jit(solution)/shard_map/pallas_call | solution.py:242
  123.4 1.6 %maximum_bitcast_fusion = bf16[1,4,1,256,2,128]{5,4,3,2,1,0:T(2,128)(2,1)} fusion(bf16[1,2,256,128]{3,1,2,0:T(2,128)(2,1)S(1)} %copy.33, bf16[2,2,256,128]{3,1,2,0:T(2,128)(2,1)S(1)} %copy.27, bf16[1,2,256,128]{3,1,2,0:T(2,128)(2,1)S(1)} %copy.32), kind=kLoop, calls=%fused_computation.2 | loop fusion | flops 524288 | bytes 1048576 | tf_op jit(solution)/shard_map/broadcast_in_dim | solution.py:372
  125.0 2.3 %shard_map.85 = (f32[2,9,64,256]{3,2,1,0:T(8,128)}, f32[2,9,64,256]{3,2,1,0:T(8,128)}) custom-call(s32[3]{0:T(128)S(1)} %pad_add_fusion.place, bf16[2,6,256,128]{3,2,1,0:T(8,128)(2,1)S(1)} %get-tuple-element.124.padded, bf16[2,2,256,128]{3,2,1,0:T(8,128)(2,1)S(1)} %collective-permute-done.40.refs_0_, ...), custom_call_target="tpu_custom_call" | custom-call | flops 1207959552 | bytes 4849676 | tf_op jit(solution)/shard_map/pallas_call | solution.py:242
  127.2 2.3 %shard_map.86 = (f32[2,9,64,256]{3,2,1,0:T(8,128)}, f32[2,9,64,256]{3,2,1,0:T(8,128)}) custom-call(s32[3]{0:T(128)S(1)} %pad_add_fusion.place, bf16[2,6,256,128]{3,2,1,0:T(8,128)(2,1)S(1)} %get-tuple-element.112.padded, bf16[2,384,128]{2,1,0:T(8,128)(2,1)S(1)} %collective-permute-done.38.refs_0_, ...), custom_call_target="tpu_custom_call", output_to_operand_aliasing={{0}: (6, {}), {1}: (7, {})} | custom-call | flops 1207959552 | bytes 7077900 | tf_op jit(solution)/shard_map/pallas_call | solution.py:242
  (113 shorter events, 39.1 us)
Async XLA Ops:
  2.9 8.0 %collective-permute-start.6 = (bf16[9,64,256]{2,1,0:T(8,128)(2,1)S(1)}, bf16[9,64,256]{2,1,0:T(8,128)(2,1)S(1)}, u32[]{:S(2)}, u32[]{:S(2)}) collective-permute-start(bf16[9,64,256]{2,1,0:T(8,128)(2,1)S(1)} %fusion.1.refs_0_), channel_id=1, source_target_pairs={{2,0},{0,2},{3,1},{1,3},{6,4},{4,6},{7,5},{5,7},{10,8},{8,10},{11,... | collective-permute-start | bytes 884744 | tf_op jit(solution)/shard_map/ppermute | solution.py:29
  4.2 19.0 %collective-permute-start.5 = (bf16[9,64,256]{2,1,0:T(8,128)(2,1)S(1)}, bf16[9,64,256]{2,1,0:T(8,128)(2,1)S(1)}, u32[]{:S(2)}, u32[]{:S(2)}) collective-permute-start(bf16[9,64,256]{2,1,0:T(8,128)(2,1)S(1)} %fusion.1.refs_0_), channel_id=1, source_target_pairs={{1,0},{0,1},{3,2},{2,3},{5,4},{4,5},{7,6},{6,7},{9,8},{8,9},{11,10... | collective-permute-start | bytes 884744 | tf_op jit(solution)/shard_map/ppermute | solution.py:29
  5.2 12.0 %collective-permute-start.3 = (bf16[9,64,256]{2,1,0:T(8,128)(2,1)S(1)}, bf16[9,64,256]{2,1,0:T(8,128)(2,1)S(1)}, u32[]{:S(2)}, u32[]{:S(2)}) collective-permute-start(bf16[9,64,256]{2,1,0:T(8,128)(2,1)S(1)} %fusion.refs_0_), channel_id=1, source_target_pairs={{2,0},{0,2},{3,1},{1,3},{6,4},{4,6},{7,5},{5,7},{10,8},{8,10},{11,... | collective-permute-start | bytes 884744 | tf_op jit(solution)/shard_map/ppermute | solution.py:29
  5.4 13.3 %collective-permute-start.2 = (bf16[9,64,256]{2,1,0:T(8,128)(2,1)S(1)}, bf16[9,64,256]{2,1,0:T(8,128)(2,1)S(1)}, u32[]{:S(2)}, u32[]{:S(2)}) collective-permute-start(bf16[9,64,256]{2,1,0:T(8,128)(2,1)S(1)} %fusion.refs_0_), channel_id=1, source_target_pairs={{1,0},{0,1},{3,2},{2,3},{5,4},{4,5},{7,6},{6,7},{9,8},{8,9},{11,10... | collective-permute-start | bytes 884744 | tf_op jit(solution)/shard_map/ppermute | solution.py:29
  6.9 18.5 %collective-permute-start.1 = (bf16[2,2,256,128]{3,2,1,0:T(8,128)(2,1)}, bf16[2,2,256,128]{3,2,1,0:T(8,128)(2,1)}, u32[]{:S(2)}, u32[]{:S(2)}) collective-permute-start(bf16[2,2,256,128]{3,2,1,0:T(8,128)(2,1)} %pad_maximum_fusion.1.refs_2_), channel_id=1, source_target_pairs={{1,0},{0,1},{3,2},{2,3},{5,4},{4,5},{7,6},{6,7},{9,8},{8,9},{11,10... | collective-permute-start | bytes 786440 | tf_op jit(solution)/shard_map/ppermute | solution.py:29
  10.9 15.8 %collective-permute-start = (bf16[2,2,256,128]{3,2,1,0:T(8,128)(2,1)S(1)}, bf16[2,2,256,128]{3,2,1,0:T(8,128)(2,1)}, u32[]{:S(2)}, u32[]{:S(2)}) collective-permute-start(bf16[2,2,256,128]{3,2,1,0:T(8,128)(2,1)S(1)} %pad_maximum_fusion.refs_0_.first), channel_id=1, source_target_pairs={{1,0},{0,1},{3,2},{2,3},{5,4},{4,5},{7,6},{6,7},{9,8},{8,9},{11,10... | collective-permute-start | bytes 786440 | tf_op jit(solution)/shard_map/ppermute | solution.py:29
  20.5 13.4 %collective-permute-start.12 = (bf16[2,2,256,128]{3,2,1,0:T(8,128)(2,1)S(1)}, bf16[2,2,256,128]{3,2,1,0:T(8,128)(2,1)S(1)}, u32[]{:S(2)}, u32[]{:S(2)}) collective-permute-start(bf16[2,2,256,128]{3,2,1,0:T(8,128)(2,1)S(1)} %pad_maximum_fusion.refs_0_.first), channel_id=1, source_target_pairs={{2,0},{0,2},{3,1},{1,3},{6,4},{4,6},{7,5},{5,7},{10,8},{8,10},{11,... | collective-permute-start | bytes 786440 | tf_op jit(solution)/shard_map/ppermute | solution.py:29
  23.2 13.8 %collective-permute-start.20 = (bf16[9,64,256]{2,1,0:T(8,128)(2,1)S(1)}, bf16[9,64,256]{2,1,0:T(8,128)(2,1)S(1)}, u32[]{:S(2)}, u32[]{:S(2)}) collective-permute-start(bf16[9,64,256]{2,1,0:T(8,128)(2,1)S(1)} %get-tuple-element.143.refs_0_), channel_id=1, source_target_pairs={{2,0},{0,2},{3,1},{1,3},{6,4},{4,6},{7,5},{5,7},{10,8},{8,10},{11,... | collective-permute-start | bytes 884744 | tf_op jit(solution)/shard_map/ppermute | solution.py:29
  23.5 20.1 %collective-permute-start.19 = (bf16[9,64,256]{2,1,0:T(8,128)(2,1)S(1)}, bf16[9,64,256]{2,1,0:T(8,128)(2,1)S(1)}, u32[]{:S(2)}, u32[]{:S(2)}) collective-permute-start(bf16[9,64,256]{2,1,0:T(8,128)(2,1)S(1)} %get-tuple-element.143.refs_0_), channel_id=1, source_target_pairs={{1,0},{0,1},{3,2},{2,3},{5,4},{4,5},{7,6},{6,7},{9,8},{8,9},{11,10... | collective-permute-start | bytes 884744 | tf_op jit(solution)/shard_map/ppermute | solution.py:29
  25.5 18.2 %collective-permute-start.15 = (bf16[9,64,256]{2,1,0:T(8,128)(2,1)S(1)}, bf16[9,64,256]{2,1,0:T(8,128)(2,1)S(1)}, u32[]{:S(2)}, u32[]{:S(2)}) collective-permute-start(bf16[9,64,256]{2,1,0:T(8,128)(2,1)S(1)} %get-tuple-element.144.refs_0_), channel_id=1, source_target_pairs={{2,0},{0,2},{3,1},{1,3},{6,4},{4,6},{7,5},{5,7},{10,8},{8,10},{11,... | collective-permute-start | bytes 884744 | tf_op jit(solution)/shard_map/ppermute | solution.py:29
  31.3 10.4 %collective-permute-start.8 = (bf16[2,2,256,128]{3,2,1,0:T(8,128)(2,1)S(1)}, bf16[2,2,256,128]{3,2,1,0:T(8,128)(2,1)S(1)}, u32[]{:S(2)}, u32[]{:S(2)}) collective-permute-start(bf16[2,2,256,128]{3,2,1,0:T(8,128)(2,1)S(1)} %shard_map.70), channel_id=1, source_target_pairs={{4,0},{8,4},{12,8},{16,12},{20,16},{24,20},{28,24},{5,1},{9,5},{13... | collective-permute-start | bytes 786440 | tf_op jit(solution)/shard_map/ppermute | solution.py:365
  33.9 13.4 %collective-permute-start.10 = (bf16[2,2,256,128]{3,2,1,0:T(8,128)(2,1)S(1)}, bf16[2,2,256,128]{3,2,1,0:T(8,128)(2,1)S(1)}, u32[]{:S(2)}, u32[]{:S(2)}) collective-permute-start(bf16[2,2,256,128]{3,2,1,0:T(8,128)(2,1)S(1)} %get-tuple-element.72.second), channel_id=1, source_target_pairs={{4,0},{8,4},{12,8},{16,12},{20,16},{24,20},{28,24},{5,1},{9,5},{13... | collective-permute-start | bytes 786440 | tf_op jit(solution)/shard_map/ppermute | solution.py:351
  37.0 10.6 %collective-permute-start.14 = (bf16[9,64,256]{2,1,0:T(8,128)(2,1)S(1)}, bf16[9,64,256]{2,1,0:T(8,128)(2,1)S(1)}, u32[]{:S(2)}, u32[]{:S(2)}) collective-permute-start(bf16[9,64,256]{2,1,0:T(8,128)(2,1)S(1)} %get-tuple-element.144.refs_0_), channel_id=1, source_target_pairs={{1,0},{0,1},{3,2},{2,3},{5,4},{4,5},{7,6},{6,7},{9,8},{8,9},{11,10... | collective-permute-start | bytes 884744 | tf_op jit(solution)/shard_map/ppermute | solution.py:29
  41.7 7.4 %collective-permute-start.21 = (bf16[9,64,256]{2,1,0:T(8,128)(2,1)S(1)}, bf16[9,64,256]{2,1,0:T(8,128)(2,1)S(1)}, u32[]{:S(2)}, u32[]{:S(2)}) collective-permute-start(bf16[9,64,256]{2,1,0:T(8,128)(2,1)S(1)} %collective-permute-done.20.refs_2_), channel_id=1, source_target_pairs={{1,0},{0,1},{3,2},{2,3},{5,4},{4,5},{7,6},{6,7},{9,8},{8,9},{11,10... | collective-permute-start | bytes 884744 | tf_op jit(solution)/shard_map/ppermute | solution.py:29
  43.6 13.7 %collective-permute-start.13 = (bf16[2,2,256,128]{3,2,1,0:T(8,128)(2,1)S(1)}, bf16[2,2,256,128]{3,2,1,0:T(8,128)(2,1)S(1)}, u32[]{:S(2)}, u32[]{:S(2)}) collective-permute-start(bf16[2,2,256,128]{3,2,1,0:T(8,128)(2,1)S(1)} %collective-permute-done.12.refs_0_), channel_id=1, source_target_pairs={{1,0},{0,1},{3,2},{2,3},{5,4},{4,5},{7,6},{6,7},{9,8},{8,9},{11,10... | collective-permute-start | bytes 786440 | tf_op jit(solution)/shard_map/ppermute | solution.py:29
  43.7 13.0 %collective-permute-start.16 = (bf16[9,64,256]{2,1,0:T(8,128)(2,1)S(1)}, bf16[9,64,256]{2,1,0:T(8,128)(2,1)S(1)}, u32[]{:S(2)}, u32[]{:S(2)}) collective-permute-start(bf16[9,64,256]{2,1,0:T(8,128)(2,1)S(1)} %collective-permute-done.15.refs_2_), channel_id=1, source_target_pairs={{1,0},{0,1},{3,2},{2,3},{5,4},{4,5},{7,6},{6,7},{9,8},{8,9},{11,10... | collective-permute-start | bytes 884744 | tf_op jit(solution)/shard_map/ppermute | solution.py:29
  47.6 13.2 %collective-permute-start.11 = (bf16[2,2,256,128]{3,2,1,0:T(8,128)(2,1)S(1)}, bf16[2,2,256,128]{3,2,1,0:T(8,128)(2,1)S(1)}, u32[]{:S(2)}, u32[]{:S(2)}) collective-permute-start(bf16[2,2,256,128]{3,2,1,0:T(8,128)(2,1)S(1)} %broadcast_select_fusion.4.refs_2_), channel_id=1, source_target_pairs={{1,0},{0,1},{3,2},{2,3},{5,4},{4,5},{7,6},{6,7},{9,8},{8,9},{11,10... | collective-permute-start | bytes 786440 | tf_op jit(solution)/shard_map/ppermute | solution.py:29
  49.1 11.8 %collective-permute-start.9 = (bf16[2,2,256,128]{3,2,1,0:T(8,128)(2,1)S(1)}, bf16[2,2,256,128]{3,2,1,0:T(8,128)(2,1)S(1)}, u32[]{:S(2)}, u32[]{:S(2)}) collective-permute-start(bf16[2,2,256,128]{3,2,1,0:T(8,128)(2,1)S(1)} %broadcast_select_fusion.5.refs_0_.first), channel_id=1, source_target_pairs={{1,0},{0,1},{3,2},{2,3},{5,4},{4,5},{7,6},{6,7},{9,8},{8,9},{11,10... | collective-permute-start | bytes 786440 | tf_op jit(solution)/shard_map/ppermute | solution.py:29
  54.0 12.7 %collective-permute-start.18 = (bf16[2,2,256,128]{3,2,1,0:T(8,128)(2,1)S(1)}, bf16[2,2,256,128]{3,2,1,0:T(8,128)(2,1)S(1)}, u32[]{:S(2)}, u32[]{:S(2)}) collective-permute-start(bf16[2,2,256,128]{3,2,1,0:T(8,128)(2,1)S(1)} %collective-permute-done.17.refs_0_), channel_id=1, source_target_pairs={{1,0},{0,1},{3,2},{2,3},{5,4},{4,5},{7,6},{6,7},{9,8},{8,9},{11,10... | collective-permute-start | bytes 786440 | tf_op jit(solution)/shard_map/ppermute | solution.py:29
  60.5 14.0 %collective-permute-start.26 = (bf16[2,2,256,128]{3,2,1,0:T(8,128)(2,1)S(1)}, bf16[2,2,256,128]{3,2,1,0:T(8,128)(2,1)S(1)}, u32[]{:S(2)}, u32[]{:S(2)}) collective-permute-start(bf16[2,2,256,128]{3,2,1,0:T(8,128)(2,1)S(1)} %broadcast_select_fusion.5.refs_0_.first), channel_id=1, source_target_pairs={{2,0},{0,2},{3,1},{1,3},{6,4},{4,6},{7,5},{5,7},{10,8},{8,10},{11,... | collective-permute-start | bytes 786440 | tf_op jit(solution)/shard_map/ppermute | solution.py:29
  63.3 12.9 %collective-permute-start.28 = (bf16[2,2,256,128]{3,2,1,0:T(8,128)(2,1)S(1)}, bf16[2,2,256,128]{3,2,1,0:T(8,128)(2,1)S(1)}, u32[]{:S(2)}, u32[]{:S(2)}) collective-permute-start(bf16[2,2,256,128]{3,2,1,0:T(8,128)(2,1)S(1)} %get-tuple-element.83.second), channel_id=1, source_target_pairs={{2,0},{0,2},{3,1},{1,3},{6,4},{4,6},{7,5},{5,7},{10,8},{8,10},{11,... | collective-permute-start | bytes 786440 | tf_op jit(solution)/shard_map/ppermute | solution.py:29
  64.6 11.1 %collective-permute-start.24 = (bf16[2,2,256,128]{3,2,1,0:T(8,128)(2,1)S(1)}, bf16[2,2,256,128]{3,2,1,0:T(8,128)(2,1)S(1)}, u32[]{:S(2)}, u32[]{:S(2)}) collective-permute-start(bf16[2,2,256,128]{3,2,1,0:T(8,128)(2,1)S(1)} %get-tuple-element.83.second), channel_id=1, source_target_pairs={{4,0},{8,4},{12,8},{16,12},{20,16},{24,20},{28,24},{5,1},{9,5},{13... | collective-permute-start | bytes 786440 | tf_op jit(solution)/shard_map/ppermute | solution.py:351
  70.8 10.1 %collective-permute-start.22 = (bf16[2,2,256,128]{3,2,1,0:T(8,128)(2,1)S(1)}, bf16[2,2,256,128]{3,2,1,0:T(8,128)(2,1)S(1)}, u32[]{:S(2)}, u32[]{:S(2)}) collective-permute-start(bf16[2,2,256,128]{3,2,1,0:T(8,128)(2,1)S(1)} %shard_map.76), channel_id=1, source_target_pairs={{4,0},{8,4},{12,8},{16,12},{20,16},{24,20},{28,24},{5,1},{9,5},{13... | collective-permute-start | bytes 786440 | tf_op jit(solution)/shard_map/ppermute | solution.py:365
  74.5 8.2 %collective-permute-start.27 = (bf16[2,2,256,128]{3,2,1,0:T(8,128)(2,1)S(1)}, bf16[2,2,256,128]{3,2,1,0:T(8,128)(2,1)S(1)}, u32[]{:S(2)}, u32[]{:S(2)}) collective-permute-start(bf16[2,2,256,128]{3,2,1,0:T(8,128)(2,1)S(1)} %collective-permute-done.26.refs_0_), channel_id=1, source_target_pairs={{1,0},{0,1},{3,2},{2,3},{5,4},{4,5},{7,6},{6,7},{9,8},{8,9},{11,10... | collective-permute-start | bytes 786440 | tf_op jit(solution)/shard_map/ppermute | solution.py:29
  75.7 12.1 %collective-permute-start.25 = (bf16[2,2,256,128]{3,2,1,0:T(8,128)(2,1)S(1)}, bf16[2,2,256,128]{3,2,1,0:T(8,128)(2,1)S(1)}, u32[]{:S(2)}, u32[]{:S(2)}) collective-permute-start(bf16[2,2,256,128]{3,2,1,0:T(8,128)(2,1)S(1)} %broadcast_select_fusion.2.refs_2_), channel_id=1, source_target_pairs={{1,0},{0,1},{3,2},{2,3},{5,4},{4,5},{7,6},{6,7},{9,8},{8,9},{11,10... | collective-permute-start | bytes 786440 | tf_op jit(solution)/shard_map/ppermute | solution.py:29
  76.2 9.1 %collective-permute-start.29 = (bf16[2,2,256,128]{3,2,1,0:T(8,128)(2,1)S(1)}, bf16[2,2,256,128]{3,2,1,0:T(8,128)(2,1)S(1)}, u32[]{:S(2)}, u32[]{:S(2)}) collective-permute-start(bf16[2,2,256,128]{3,2,1,0:T(8,128)(2,1)S(1)} %collective-permute-done.28.refs_0_), channel_id=1, source_target_pairs={{1,0},{0,1},{3,2},{2,3},{5,4},{4,5},{7,6},{6,7},{9,8},{8,9},{11,10... | collective-permute-start | bytes 786440 | tf_op jit(solution)/shard_map/ppermute | solution.py:29
  82.4 16.6 %collective-permute-start.34 = (bf16[2,2,256,128]{3,2,1,0:T(8,128)(2,1)S(1)}, bf16[2,2,256,128]{3,2,1,0:T(8,128)(2,1)S(1)}, u32[]{:S(2)}, u32[]{:S(2)}) collective-permute-start(bf16[2,2,256,128]{3,2,1,0:T(8,128)(2,1)S(1)} %broadcast_select_fusion.3.refs_0_.first), channel_id=1, source_target_pairs={{2,0},{0,2},{3,1},{1,3},{6,4},{4,6},{7,5},{5,7},{10,8},{8,10},{11,... | collective-permute-start | bytes 786440 | tf_op jit(solution)/shard_map/ppermute | solution.py:29
  91.9 17.2 %collective-permute-start.30 = (bf16[2,2,256,128]{3,2,1,0:T(8,128)(2,1)S(1)}, bf16[2,2,256,128]{3,2,1,0:T(8,128)(2,1)S(1)}, u32[]{:S(2)}, u32[]{:S(2)}) collective-permute-start(bf16[2,2,256,128]{3,2,1,0:T(8,128)(2,1)S(1)} %shard_map.80), channel_id=1, source_target_pairs={{4,0},{8,4},{12,8},{16,12},{20,16},{24,20},{28,24},{5,1},{9,5},{13... | collective-permute-start | bytes 786440 | tf_op jit(solution)/shard_map/ppermute | solution.py:365
  94.2 15.0 %collective-permute-start.36 = (bf16[2,2,256,128]{3,2,1,0:T(8,128)(2,1)S(1)}, bf16[2,2,256,128]{3,2,1,0:T(8,128)(2,1)S(1)}, u32[]{:S(2)}, u32[]{:S(2)}) collective-permute-start(bf16[2,2,256,128]{3,2,1,0:T(8,128)(2,1)S(1)} %get-tuple-element.97.second), channel_id=1, source_target_pairs={{2,0},{0,2},{3,1},{1,3},{6,4},{4,6},{7,5},{5,7},{10,8},{8,10},{11,... | collective-permute-start | bytes 786440 | tf_op jit(solution)/shard_map/ppermute | solution.py:29
  95.5 12.3 %collective-permute-start.32 = (bf16[2,2,256,128]{3,2,1,0:T(8,128)(2,1)S(1)}, bf16[2,2,256,128]{3,2,1,0:T(8,128)(2,1)S(1)}, u32[]{:S(2)}, u32[]{:S(2)}) collective-permute-start(bf16[2,2,256,128]{3,2,1,0:T(8,128)(2,1)S(1)} %get-tuple-element.97.second), channel_id=1, source_target_pairs={{4,0},{8,4},{12,8},{16,12},{20,16},{24,20},{28,24},{5,1},{9,5},{13... | collective-permute-start | bytes 786440 | tf_op jit(solution)/shard_map/ppermute | solution.py:351
  99.0 11.9 %collective-permute-start.35 = (bf16[2,2,256,128]{3,2,1,0:T(8,128)(2,1)S(1)}, bf16[2,2,256,128]{3,2,1,0:T(8,128)(2,1)S(1)}, u32[]{:S(2)}, u32[]{:S(2)}) collective-permute-start(bf16[2,2,256,128]{3,2,1,0:T(8,128)(2,1)S(1)} %collective-permute-done.34.refs_0_), channel_id=1, source_target_pairs={{1,0},{0,1},{3,2},{2,3},{5,4},{4,5},{7,6},{6,7},{9,8},{8,9},{11,10... | collective-permute-start | bytes 786440 | tf_op jit(solution)/shard_map/ppermute | solution.py:29
  109.7 11.0 %collective-permute-start.40 = (bf16[2,2,256,128]{3,2,1,0:T(8,128)(2,1)S(1)}, bf16[2,2,256,128]{3,2,1,0:T(8,128)(2,1)S(1)}, u32[]{:S(2)}, u32[]{:S(2)}) collective-permute-start(bf16[2,2,256,128]{3,2,1,0:T(8,128)(2,1)S(1)} %broadcast_select_fusion.1.refs_0_.first), channel_id=1, source_target_pairs={{2,0},{0,2},{3,1},{1,3},{6,4},{4,6},{7,5},{5,7},{10,8},{8,10},{11,... | collective-permute-start | bytes 786440 | tf_op jit(solution)/shard_map/ppermute | solution.py:29
  (14 other events, 65.9 us)
